TPU v7x, 256 devices: a whole 4x4x8 slice. The times are simulated.
256 devices in a mesh: dev: 128 (over z, y, x), rep: 2 (over core).
Axes of the slice: x: 4, y: 4, z: 8, core: 2. Of those that a mesh axis runs over, the one named last changes fastest.
Arguments:
- tables: bfloat16 [512, 2048, 128], P('dev'), may hold values from -1.5 to 1.5
- bag_rows: int32 [256, 512, 32, 4], P(('rep', 'dev')), parts along dimension 0, may hold values from 0 to 2047
- bag_lengths: int32 [256, 512, 32], P(('rep', 'dev')), parts along dimension 0, may hold values from 1 to 4
- row_counts: int32 [256, 512], P(('rep', 'dev')), parts along dimension 0, may hold values from 1 to 32, as said below
- inverse: int32 [32768, 512], P(('rep', 'dev')), parts along dimension 0, may hold values from 0 to 31
- table_order: int32 [512], replicated, may hold values from 0 to 511, each once
- compress: bfloat16 [16, 512], replicated, may hold values from -0.25 to 0.25
- top_weight: bfloat16 [8192, 512], replicated, may hold values from -0.0625 to 0.0625
- top_bias: float32 [512], replicated, may hold values from -1.8 to 1.8
Outputs:
- ranked: bfloat16 [32768, 512], P(('rep', 'dev')), parts along dimension 0
There are 2 independent parts, one for each index of `rep`. A program takes and returns all parts, laid end to end along the dimension named above; an argument that names none is the same for every part. Nothing has to cross between parts.
Inputs may be any that keep to these rules, and one draw needn't show every extreme that they name: `row_counts`: for every sample device and every aligned group of 4 consecutive slots the counts sum to at most 80; a count of 32 and a group sum of 80 occur in every draw.
All inputs are finite; a program needn't handle non-finite values.
Results may differ from a plain program's by a relative error of at most 0.0062.
Values may be sent and summed in bfloat16 or wider, within the bound.
No kernel may reach another device: no remote copies, remote signals or barrier semaphores. Data moves between devices by JAX's collectives and lax.ppermute only.
A program may use at most 128 MiB of HBM per device.

v0:
```python
import math

import jax
import jax.numpy as jnp
from jax import lax
from jax.sharding import PartitionSpec as P


def pool_bags(tables, bag_ids, bag_lens):
    vocabulary = tables.shape[1]
    table_rows = tables.reshape(-1, tables.shape[2])
    offsets = jnp.arange(tables.shape[0], dtype=jnp.int32) * vocabulary
    wanted = bag_ids + offsets[None, :, None, None]
    picked = jnp.take(table_rows, wanted, axis=0, mode="clip")
    places = jnp.arange(bag_ids.shape[3], dtype=jnp.int32)
    active = places[None, None, None, :] < bag_lens[..., None]
    summed = jnp.sum(jnp.where(active[..., None], picked.astype(jnp.float32), 0.0), axis=3)
    return summed.astype(jnp.bfloat16)


def shards(
    tables, bag_rows, bag_lengths, row_counts, inverse, table_order, compress, top_weight, top_bias
):
    width_emb = tables.shape[2]
    total_slots = table_order.shape[0]
    most_rows = bag_rows.shape[2]
    my_counts = row_counts[0]
    got_rows, got_lengths = (
        lax.all_to_all(bag_rows, "dev", split_axis=1, concat_axis=0, tiled=True),
        lax.all_to_all(bag_lengths, "dev", split_axis=1, concat_axis=0, tiled=True),
    )
    pooled = pool_bags(tables, got_rows, got_lengths)
    arrived = lax.all_to_all(pooled, "dev", split_axis=0, concat_axis=1, tiled=True).reshape(
        -1, width_emb
    )
    slot_base = jnp.arange(total_slots, dtype=jnp.int32) * most_rows
    slot_range = jnp.arange(total_slots, dtype=jnp.int32)
    matches = table_order[:, None] == slot_range[None, :]
    feature_base = jnp.sum(jnp.where(matches, slot_base[:, None], 0), axis=0)
    feature_count = jnp.sum(jnp.where(matches, my_counts[:, None], 0), axis=0)
    row_range = jnp.arange(most_rows, dtype=jnp.int32)
    feature_rows = jnp.take(
        arrived, feature_base[:, None] + row_range[None, :], axis=0, mode="clip"
    )
    samples = inverse.shape[0]
    block_rows = math.gcd(samples, 128)

    def score_block(inverse_block):
        present = inverse_block < feature_count[None, :]
        selector = (inverse_block[..., None] == row_range[None, None, :]) & present[..., None]
        selector = selector.astype(jnp.bfloat16)
        features = jnp.einsum(
            "bfu,fue->bfe", selector, feature_rows, preferred_element_type=jnp.float32
        ).astype(jnp.bfloat16)
        mixed = jnp.einsum(
            "kf,bfe->bke", compress, features, preferred_element_type=jnp.float32
        ).astype(jnp.bfloat16)
        pairwise = jnp.einsum(
            "bfe,bke->bfk", features, mixed, preferred_element_type=jnp.float32
        ).astype(jnp.bfloat16)
        hidden_pre = (
            jnp.dot(
                pairwise.reshape(pairwise.shape[0], -1),
                top_weight,
                preferred_element_type=jnp.float32,
            )
            + top_bias
        )
        return jnp.maximum(hidden_pre, 0.0).astype(jnp.bfloat16)

    ranked = lax.map(score_block, inverse.reshape(samples // block_rows, block_rows, total_slots))
    return ranked.reshape(samples, -1)


def solution(mesh):
    return jax.shard_map(
        shards,
        mesh=mesh,
        in_specs=(
            P("dev", None, None),
            P(("rep", "dev"), None, None, None),
            P(("rep", "dev"), None, None),
            P(("rep", "dev"), None),
            P(("rep", "dev"), None),
            P(),
            P(),
            P(),
            P(),
        ),
        out_specs=P(("rep", "dev"), None),
        check_vma=False,
    )
```

profile of v0, /device:TPU:32, one launch (start us, length us, event | category | flops | bytes accessed | tf_op | source)
XLA Modules:
  0.0 546.3 jit_solution(15885233483454164998)
XLA Ops:
  0.0 0.0 copy-start
  0.0 1.1 copy.39
  1.1 0.6 broadcast.69
  1.7 1.3 reduce.1
  3.0 0.8 reshape.111
  3.8 15.0 %all-to-all-start = ((s32[128,1,128]{2,1,0:T(1,128)}), s32[128,1,128]{2,1,0:T(1,128)S(1)}, u32[]{:S(2)}, u32[]{:S(2)}) async-start(s32[128,1,128]{2,1,0:T(1,128)} %reshape.111), calls=%async_computation | async-start | bytes 131072 | tf_op jit(solution)/shard_map/all_to_all | solution.py:30
  18.8 1.4 copy.40
  20.1 1.4 reshape.109
  21.5 8.7 %all-to-all-done = s32[128,1,128]{2,1,0:T(1,128)S(1)} async-done(((s32[128,1,128]{2,1,0:T(1,128)}), s32[128,1,128]{2,1,0:T(1,128)S(1)}, u32[]{:S(2)}, u32[]{:S(2)}) %all-to-all-start) | async-done | bytes 65568 | tf_op jit(solution)/shard_map/all_to_all | solution.py:30
  30.2 6.6 %all-to-all-start.1 = ((s32[128,1,512]{2,1,0:T(1,128)}), s32[128,1,512]{2,1,0:T(1,128)S(1)}, u32[]{:S(2)}, u32[]{:S(2)}) async-start(s32[128,1,512]{2,1,0:T(1,128)} %reshape.109), calls=%async_computation.1 | async-start | bytes 524288 | tf_op jit(solution)/shard_map/all_to_all | solution.py:29
  36.8 0.8 reduce.2
  37.6 0.4 reshape.112
  38.0 4.6 iota_compare_fusion.1
  42.6 7.8 %all-to-all-done.1 = s32[128,1,512]{2,1,0:T(1,128)S(1)} async-done(((s32[128,1,512]{2,1,0:T(1,128)}), s32[128,1,512]{2,1,0:T(1,128)S(1)}, u32[]{:S(2)}, u32[]{:S(2)}) %all-to-all-start.1) | async-done | bytes 262176 | tf_op jit(solution)/shard_map/all_to_all | solution.py:29
  50.4 1.2 reduce
  51.7 0.5 reshape.110
  52.2 0.1 copy.41
  52.3 0.2 broadcast_add_fusion
  52.5 5.2 copy.42
  57.8 8.2 %reshape.91 = s32[65536]{0:T(1024)S(1)} reshape(s32[128,4,32,4,1]{3,2,1,0,4:T(8,128)} %copy.42) | data formatting | bytes 524288 | tf_op jit(solution)/shard_map/add | solution.py:13
  66.0 0.0 copy-done
  66.0 227.3 %gather_fusion = bf16[65536,128]{1,0:T(8,128)(2,1)} fusion(bf16[8192,128]{1,0:T(8,128)(2,1)S(1)} %bitcast.30, s32[65536]{0:T(1024)S(1)} %broadcast_clamp_fusion), kind=kCustom, calls=%fused_computation | custom fusion | bytes 33816576 | tf_op jit(solution)/shard_map/jit(_take)/gather | solution.py:14
  293.3 35.9 %fusion = bf16[128,4,32,128]{3,2,1,0:T(8,128)(2,1)} fusion(bf16[128,4,32,4,128]{4,3,2,1,0:T(4,128)(2,1)} %bitcast.31, pred[128,4,32,4]{3,2,1,0:T(8,128)(4,1)} %iota_compare_fusion.1), kind=kLoop, calls=%fused_computation.3 | loop fusion | flops 23068672 | bytes 21037056 | tf_op jit(solution)/shard_map/reduce_sum | solution.py:17
  329.3 0.0 copy-start.2
  329.3 0.0 copy-start.5
  329.3 0.0 copy-start.6
  329.3 7.8 %all-to-all-start.2 = ((bf16[128,4,32,128]{3,2,1,0:T(8,128)(2,1)}), bf16[128,4,32,128]{3,2,1,0:T(8,128)(2,1)}, u32[]{:S(2)}, u32[]{:S(2)}) async-start(bf16[128,4,32,128]{3,2,1,0:T(8,128)(2,1)} %fusion), calls=%async_computation.2 | async-start | bytes 8388608 | tf_op jit(solution)/shard_map/all_to_all | solution.py:33
  337.1 0.0 copy-done.2
  337.1 0.1 copy.43
  337.2 0.0 copy-done.5
  337.2 0.0 copy-done.6
  337.3 0.3 select_reduce_fusion
  337.6 0.2 copy.44
  337.8 0.1 iota_add_fusion
  337.9 0.1 reshape.99
  338.0 92.4 %all-to-all-done.2 = bf16[128,4,32,128]{3,2,1,0:T(8,128)(2,1)} async-done(((bf16[128,4,32,128]{3,2,1,0:T(8,128)(2,1)}), bf16[128,4,32,128]{3,2,1,0:T(8,128)(2,1)}, u32[]{:S(2)}, u32[]{:S(2)}) %all-to-all-start.2) | async-done | bytes 4194336 | tf_op jit(solution)/shard_map/all_to_all | solution.py:33
  430.5 57.6 %gather_fusion.1 = bf16[16384,128]{1,0:T(8,128)(2,1)} fusion(bf16[16384,128]{1,0:T(8,128)(2,1)} %bitcast.4, s32[16384]{0:T(1024)S(1)} %broadcast_clamp_fusion.1), kind=kCustom, calls=%fused_computation.1 | custom fusion | bytes 8454144 | tf_op jit(solution)/shard_map/jit(_take)/gather | solution.py:42
  488.1 9.8 %convert_bitcast_fusion = bf16[128,512,128]{0,2,1:T(8,128)(2,1)} fusion(bf16[512,32,128]{2,1,0:T(8,128)(2,1)} %bitcast.32, s32[128,512]{0,1:T(8,128)S(1)} %copy.43, pred[128,512]{0,1:T(8,128)(4,1)S(1)} %copy.44), kind=kOutput, calls=%fused_computation.4 | convolution fusion | flops 549453824 | bytes 21299200 | tf_op jit(solution)/shard_map/while/body/eval_jaxpr/bfu,fue->bfe/dot_general | solution.py:52
  497.9 0.0 copy-start.3
  497.9 21.5 %copy.46 = bf16[128,512,128]{2,1,0:T(8,128)(2,1)} copy(bf16[128,512,128]{0,2,1:T(8,128)(2,1)} %convert_bitcast_fusion) | data formatting | bytes 33554432 | tf_op jit(solution)/shard_map/while/body/eval_jaxpr/convert_element_type | solution.py:54
  519.4 0.0 copy-done.3
  519.4 0.0 copy-start.4
  519.4 16.9 %convolution_convert_fusion = bf16[128,512,16]{1,2,0:T(8,128)(2,1)S(1)} fusion(bf16[128,512,128]{2,1,0:T(8,128)(2,1)} %copy.46, bf16[16,512]{1,0:T(8,128)(2,1)S(1)} %copy-done.3), kind=kOutput, calls=%fused_computation.10 | convolution fusion | flops 538181632 | bytes 18890752 | tf_op jit(solution)/shard_map/while/body/eval_jaxpr/bfe,bke->bfk/dot_general | solution.py:58
  536.2 3.9 copy.47
  540.1 0.0 copy-start.1
  540.1 0.0 copy-done.4
  540.1 6.1 %fusion.6 = bf16[128,512]{1,0:T(8,128)(2,1)} fusion(bf16[128,8192]{0,1:T(8,128)(2,1)} %bitcast.33, bf16[8192,512]{1,0:T(8,128)(2,1)} %param.16, f32[512]{0:T(512)S(1)} %copy-done.4), kind=kOutput, calls=%fused_computation.14 | convolution fusion | flops 1073938432 | bytes 10618880 | tf_op jit(solution)/shard_map/while/body/eval_jaxpr/dot_general | solution.py:62
  546.3 0.0 copy-done.1
  (5 shorter events, 0.1 us)
Async XLA Ops:
  0.0 66.0 %copy-start = (bf16[4,2048,128]{2,1,0:T(8,128)(2,1)S(1)}, bf16[4,2048,128]{2,1,0:T(8,128)(2,1)}, u32[]{:S(2)}) copy-start(bf16[4,2048,128]{2,1,0:T(8,128)(2,1)} %param.9) | copy-start | bytes 6291460
  3.8 26.4 %all-to-all-start = ((s32[128,1,128]{2,1,0:T(1,128)}), s32[128,1,128]{2,1,0:T(1,128)S(1)}, u32[]{:S(2)}, u32[]{:S(2)}) async-start(s32[128,1,128]{2,1,0:T(1,128)} %reshape.111), calls=%async_computation | async-start | bytes 131072 | tf_op jit(solution)/shard_map/all_to_all | solution.py:30
  30.2 20.3 %all-to-all-start.1 = ((s32[128,1,512]{2,1,0:T(1,128)}), s32[128,1,512]{2,1,0:T(1,128)S(1)}, u32[]{:S(2)}, u32[]{:S(2)}) async-start(s32[128,1,512]{2,1,0:T(1,128)} %reshape.109), calls=%async_computation.1 | async-start | bytes 524288 | tf_op jit(solution)/shard_map/all_to_all | solution.py:29
  329.3 7.8 %copy-start.2 = (s32[128,512]{1,0:T(8,128)S(1)}, s32[128,512]{1,0:T(8,128)}, u32[]{:S(2)}) copy-start(s32[128,512]{1,0:T(8,128)} %param.13) | copy-start | bytes 786436
  329.3 8.0 %copy-start.5 = (s32[1,512]{1,0:T(1,128)S(1)}, s32[1,512]{1,0:T(1,128)}, u32[]{:S(2)}) copy-start(s32[1,512]{1,0:T(1,128)} %param.12) | copy-start | bytes 6148
  329.3 8.0 %copy-start.6 = (s32[512]{0:T(512)S(1)}, s32[512]{0:T(512)}, u32[]{:S(2)}) copy-start(s32[512]{0:T(512)} %param.14) | copy-start | bytes 6148
  329.3 101.2 %all-to-all-start.2 = ((bf16[128,4,32,128]{3,2,1,0:T(8,128)(2,1)}), bf16[128,4,32,128]{3,2,1,0:T(8,128)(2,1)}, u32[]{:S(2)}, u32[]{:S(2)}) async-start(bf16[128,4,32,128]{3,2,1,0:T(8,128)(2,1)} %fusion), calls=%async_computation.2 | async-start | bytes 8388608 | tf_op jit(solution)/shard_map/all_to_all | solution.py:33
  497.9 21.5 %copy-start.3 = (bf16[16,512]{1,0:T(8,128)(2,1)S(1)}, bf16[16,512]{1,0:T(8,128)(2,1)}, u32[]{:S(2)}) copy-start(bf16[16,512]{1,0:T(8,128)(2,1)} %param.15) | copy-start | bytes 49156
  519.4 20.8 %copy-start.4 = (f32[512]{0:T(512)S(1)}, f32[512]{0:T(512)}, u32[]{:S(2)}) copy-start(f32[512]{0:T(512)} %param.17) | copy-start | bytes 6148
  540.1 6.1 %copy-start.1 = (bf16[4,2048,128]{2,1,0:T(8,128)(2,1)S(1)}, bf16[4,2048,128]{2,1,0:T(8,128)(2,1)}, u32[]{:S(2)}) copy-start(bf16[4,2048,128]{2,1,0:T(8,128)(2,1)} %param.9) | copy-start | bytes 6291460
where the time goes:
time: 547 us; the launch traced here: 546 us
  local copies, waits for them, and re-layouts  330 us (60%)
  waiting for transfers between devices  109 us (20%)
  other arithmetic  44.5 us (8%)
  matrix products  32.8 us (6%)
  starting transfers between devices  29.4 us (5%)
    gather x1, local copies, waits for them, and re-layouts, pool_bags(): picked = jnp.take(table_rows, wanted, axis=0, mode='clip')  227 us
    all_to_all x1, waiting for transfers between devices, shards(): lax.all_to_all(pooled, 'dev', split_axis=0, concat_axis=1, tiled=True)  92.4 us
    gather x1, local copies, waits for them, and re-layouts, shards(): jnp.take(arrived, feature_base[:, None] + row_range[None, :], axis=0, mod...  57.6 us
    reduce_sum x1, other arithmetic, pool_bags(): jnp.sum(jnp.where(active[..., None], picked.astype(jnp.float32), 0.0), ax...  35.9 us
    convert_element_type x1, local copies, waits for them, and re-layouts, score_block(): features = jnp.einsum('bfu,fue->bfe', selector, feature_rows, preferred_e...  21.5 us
    dot_general x1, matrix products, score_block(): jnp.einsum('bfe,bke->bfk', features, mixed, preferred_element_type=jnp.fl...  16.9 us
    all_to_all x1, starting transfers between devices, shards(): lax.all_to_all(bag_lengths, 'dev', split_axis=1, concat_axis=0, tiled=True)  15 us
    add x2, local copies, waits for them, and re-layouts, pool_bags(): wanted = bag_ids + offsets[None, :, None, None]  13.4 us
  transfers between devices with their start and end apart: 3, of which 3 were waited for; matrix products, arithmetic and copies ran while one was open for 2% of the time, Pallas kernels for 0%

commit v1 on v0

v1 whole, which is shorter than its diff:
```python
import functools

import jax
import jax.numpy as jnp
from jax import lax
from jax.experimental import pallas as pl
from jax.experimental.pallas import tpu as pltpu
from jax.sharding import PartitionSpec as P

PACK_ROOM = 80
GROUP = 4
UNROLL = 8


def pool_kernel(msg_ref, table_ref, out_ref, table_f32, packed, *, senders, most_rows, pool):
    vocab_rows = table_ref.shape[0]
    words = most_rows * pool // 2

    @pl.when(pl.program_id(0) == 0)
    def _():
        packed[...] = jnp.zeros_like(packed)
        table_f32[pl.ds(vocab_rows, 8), :] = jnp.zeros((8, table_f32.shape[1]), jnp.float32)

        def widen(i, carry):
            at = pl.multiple_of(i * 256, 256)
            table_f32[pl.ds(at, 256), :] = table_ref[pl.ds(at, 256), :].astype(jnp.float32)
            return carry

        lax.fori_loop(0, vocab_rows // 256, widen, 0)

    def one_sender(d, carry):
        start = jnp.int32(0)
        for slot in range(GROUP):
            count = msg_ref[d, GROUP * words + slot]

            def block(i, c, slot=slot, start=start):
                rows = []
                for r in range(UNROLL):
                    total = None
                    for h in range(pool // 2):
                        word = msg_ref[d, slot * words + h * most_rows + i * UNROLL + r]
                        low = table_f32[pl.ds(word & 0xFFFF, 1), :]
                        high = table_f32[pl.ds(lax.shift_right_logical(word, 16), 1), :]
                        part = low + high
                        total = part if total is None else total + part
                    rows.append(total)
                for r in range(UNROLL):
                    packed[pl.ds(start + i * UNROLL + r, 1), :] = rows[r]
                return c

            lax.fori_loop(0, lax.shift_right_logical(count + (UNROLL - 1), 3), block, 0)
            start = start + count
        out_ref[d] = packed[pl.ds(0, PACK_ROOM), :].astype(jnp.bfloat16)
        return carry

    lax.fori_loop(0, senders, one_sender, 0)


def pool_rows(message, table_rows, most_rows, pool):
    peers, width = message.shape
    senders = 8
    emb = table_rows.shape[1]
    return pl.pallas_call(
        functools.partial(pool_kernel, senders=senders, most_rows=most_rows, pool=pool),
        grid=(peers // senders,),
        out_shape=jax.ShapeDtypeStruct((peers, PACK_ROOM, emb), jnp.bfloat16),
        in_specs=[
            pl.BlockSpec((senders, width), lambda i: (i, 0), memory_space=pltpu.SMEM),
            pl.BlockSpec(table_rows.shape, lambda i: (0, 0)),
        ],
        out_specs=pl.BlockSpec((senders, PACK_ROOM, emb), lambda i: (i, 0, 0)),
        scratch_shapes=[
            pltpu.VMEM((table_rows.shape[0] + 8, emb), jnp.float32),
            pltpu.VMEM((PACK_ROOM + 32, emb), jnp.float32),
        ],
        compiler_params=pltpu.CompilerParams(vmem_limit_bytes=24 << 20),
        cost_estimate=pl.CostEstimate(flops=40_000_000_000, bytes_accessed=5 << 20, transcendentals=0),
    )(message, table_rows)


def tail_kernel(
    base_ref, row_ref, pos_ref, compress_ref, weight_ref, bias_ref, out_ref,
    rows_f32, feats, pairs, weight_vmem, weight_sem,
):
    total_rows, emb = row_ref.shape
    features, samples = pos_ref.shape
    mixes = compress_ref.shape[0]
    most_rows = rows_f32.shape[0] - total_rows
    copy = pltpu.make_async_copy(weight_ref, weight_vmem, weight_sem)
    copy.start()

    rows_f32[pl.ds(total_rows, most_rows), :] = jnp.zeros((most_rows, emb), jnp.float32)

    def widen(i, carry):
        at = pl.multiple_of(i * 256, 256)
        rows_f32[pl.ds(at, 256), :] = row_ref[pl.ds(at, 256), :].astype(jnp.float32)
        return carry

    lax.fori_loop(0, total_rows // 256, widen, 0)

    lane = lax.broadcasted_iota(jnp.int32, (16, 256), 1).astype(jnp.bfloat16)
    one = jnp.ones((16, 256), jnp.bfloat16)
    zero = jnp.zeros((16, 256), jnp.bfloat16)
    some = 32

    def expand(i, carry):
        at = pl.multiple_of(i * 16, 16)
        windows = []
        for half in range(2):
            parts = []
            for j in range(8):
                base = base_ref[i * 16 + half * 8 + j]
                parts.append(rows_f32[pl.ds(base, most_rows), :].astype(jnp.bfloat16))
            windows.append(jnp.concatenate(parts, axis=0))
        rhs = jnp.concatenate(windows, axis=1)
        pos = pos_ref[pl.ds(at, 16), :]
        for c in range(samples // some):
            picks = []
            for b in range(c * some, (c + 1) * some):
                wanted = jnp.broadcast_to(pos[:, b : b + 1], (16, 256))
                picks.append(jnp.where(wanted == lane, one, zero))
            lhs = jnp.concatenate(picks, axis=0)
            got = jnp.dot(lhs, rhs, preferred_element_type=jnp.float32)
            got = got.reshape(some, 2, 8, 2 * emb)
            both = jnp.concatenate([got[:, 0, :, :emb], got[:, 1, :, emb:]], axis=1)
            feats[pl.ds(c * some, some), pl.ds(at, 16), :] = both.astype(jnp.bfloat16)
        return carry

    lax.fori_loop(0, features // 16, expand, 0)

    per = 8

    def score(i, carry):
        mixing = compress_ref[...]
        stacks = []
        mixed = []
        for j in range(per // 2):
            b = i * per + 2 * j
            both = jnp.concatenate([feats[b], feats[b + 1]], axis=1)
            stacks.append(both)
            mixed.append(
                jnp.dot(mixing, both, preferred_element_type=jnp.float32).astype(jnp.bfloat16)
            )
        for j in range(per // 2):
            none = jnp.zeros((mixes, emb), jnp.bfloat16)
            first = jnp.concatenate([mixed[j][:, :emb], none], axis=1)
            second = jnp.concatenate([none, mixed[j][:, emb:]], axis=1)
            lhs = jnp.concatenate([first, second], axis=0)
            got = lax.dot_general(
                lhs, stacks[j], (((1,), (1,)), ((), ())), preferred_element_type=jnp.float32
            )
            at = pl.multiple_of((i * per + 2 * j) * mixes, 2 * mixes)
            for c in range(features // 128):
                pairs[c, pl.ds(at, 2 * mixes), :] = got[:, c * 128 : (c + 1) * 128]
        return carry

    lax.fori_loop(0, samples // per, score, 0)

    copy.wait()
    total = jnp.broadcast_to(bias_ref[...], (samples, out_ref.shape[1]))
    for k in range(mixes):
        lhs = jnp.concatenate(
            [pairs[c, pl.ds(k, samples, stride=mixes), :] for c in range(features // 128)], axis=1
        ).astype(jnp.bfloat16)
        total = total + jnp.dot(lhs, weight_vmem[k], preferred_element_type=jnp.float32)
    out_ref[...] = jnp.maximum(total, 0.0).astype(jnp.bfloat16)


def score_samples(base, rows, pos, compress, weight, bias, most_rows):
    features, samples = pos.shape
    mixes = compress.shape[0]
    units = weight.shape[2]
    emb = rows.shape[1]
    vmem = pl.BlockSpec(memory_space=pltpu.VMEM)
    return pl.pallas_call(
        tail_kernel,
        out_shape=jax.ShapeDtypeStruct((samples, units), jnp.bfloat16),
        in_specs=[
            pl.BlockSpec(memory_space=pltpu.SMEM), vmem, vmem, vmem,
            pl.BlockSpec(memory_space=pltpu.HBM), vmem,
        ],
        out_specs=vmem,
        scratch_shapes=[
            pltpu.VMEM((rows.shape[0] + most_rows, emb), jnp.float32),
            pltpu.VMEM((samples, features, emb), jnp.bfloat16),
            pltpu.VMEM((features // 128, samples * mixes, 128), jnp.float32),
            pltpu.VMEM(weight.shape, jnp.bfloat16),
            pltpu.SemaphoreType.DMA(()),
        ],
        compiler_params=pltpu.CompilerParams(vmem_limit_bytes=60 << 20),
        cost_estimate=pl.CostEstimate(flops=20_000_000_000, bytes_accessed=16 << 20, transcendentals=0),
    )(base, rows, pos, compress, weight, bias)


def bag_message(bag_rows, bag_lengths, counts, vocabulary):
    slots, most_rows, pool = bag_rows.shape
    ids = jnp.transpose(bag_rows, (1, 2, 0))
    lengths = jnp.transpose(bag_lengths, (1, 0))
    offset = (jnp.arange(slots, dtype=jnp.int32) % GROUP) * vocabulary
    spare = GROUP * vocabulary
    words = []
    for h in range(pool // 2):
        low = jnp.where(2 * h < lengths, ids[:, 2 * h, :] + offset[None, :], spare)
        high = jnp.where(2 * h + 1 < lengths, ids[:, 2 * h + 1, :] + offset[None, :], spare)
        words.append(low | (high << 16))
    packed = jnp.concatenate(words, axis=0)
    packed = jnp.transpose(packed, (1, 0)).reshape(slots // GROUP, -1)
    fill = (-(packed.shape[1] + GROUP)) % 128
    counts = jnp.pad(counts.reshape(-1, GROUP), ((0, 0), (0, fill)))
    return jnp.concatenate([packed, counts], axis=1)


def shards(
    tables, bag_rows, bag_lengths, row_counts, inverse, table_order, compress, top_weight, top_bias
):
    local_tables, vocabulary, emb = tables.shape
    slots = table_order.shape[0]
    most_rows, pool = bag_rows.shape[2:]
    mixes = compress.shape[0]
    counts = row_counts[0]
    message = bag_message(bag_rows[0], bag_lengths[0], counts, vocabulary)
    got = lax.all_to_all(message, "dev", split_axis=0, concat_axis=0, tiled=True)
    pooled = pool_rows(got, tables.reshape(-1, emb), most_rows, pool)
    arrived = lax.all_to_all(pooled, "dev", split_axis=0, concat_axis=0, tiled=True)

    grouped = counts.reshape(-1, GROUP)
    before = jnp.cumsum(grouped, axis=1) - grouped
    group_at = jnp.arange(slots // GROUP, dtype=jnp.int32)[:, None] * PACK_ROOM
    slot_base = (before + group_at).reshape(-1)
    slot_range = jnp.arange(slots, dtype=jnp.int32)
    matches = table_order[:, None] == slot_range[None, :]
    feature_base = jnp.sum(jnp.where(matches, slot_base[:, None], 0), axis=0)
    feature_count = jnp.sum(jnp.where(matches, counts[:, None], 0), axis=0)
    shift = (slot_range % 8) * most_rows
    pos = jnp.where(inverse < feature_count[None, :], inverse + shift[None, :], -1)
    pos = jnp.transpose(pos.astype(jnp.bfloat16), (1, 0))
    weight = jnp.transpose(top_weight.reshape(slots, mixes, -1), (1, 0, 2))
    return score_samples(
        feature_base, arrived.reshape(-1, emb), pos, compress, weight, top_bias[None, :], most_rows
    )


def solution(mesh):
    return jax.shard_map(
        shards,
        mesh=mesh,
        in_specs=(
            P("dev", None, None),
            P(("rep", "dev"), None, None, None),
            P(("rep", "dev"), None, None),
            P(("rep", "dev"), None),
            P(("rep", "dev"), None),
            P(),
            P(),
            P(),
            P(),
        ),
        out_specs=P(("rep", "dev"), None),
        check_vma=False,
    )
```

time: 547 us -> 220 us (0.40)
  local copies, waits for them, and re-layouts: 330 us -> 15.5 us
  Pallas kernels: 0 us -> 113 us
  waiting for transfers between devices: 109 us -> 50 us
  other arithmetic: 44.5 us -> 4.3 us
  matrix products: 32.8 us -> 0 us
  blocking collectives: 0 us -> 28.2 us
  starting transfers between devices: 29.4 us -> 7.73 us
    gather x2 -> x0, local copies, waits for them, and re-layouts: 285 us -> none  [the longest x1 227 us: pool_bags(): picked = jnp.take(table_rows, wanted, axis=0, mode='clip')]
    pallas_call x0 -> x2, Pallas kernels: none -> 113 us  [the longest x1 78.7 us: pool_rows(): pl.pallas_call(functools.partial(pool_kernel, senders=senders, most_rows=...]
    all_to_all x3 -> x1, waiting for transfers between devices: 109 us -> 50 us  [shards(): lax.all_to_all(pooled, 'dev', split_axis=0, concat_axis=0, tiled=True)]
    reduce_sum x2 -> x1, other arithmetic: 36.2 us -> 0.88 us  [shards(): feature_count = jnp.sum(jnp.where(matches, counts[:, None], 0), axis=0)]
    dot_general x3 -> x0, matrix products: 32.8 us -> none  [the longest x1 16.9 us: score_block(): jnp.einsum('bfe,bke->bfk', features, mixed, preferred_element_type=jnp.fl...]
    all_to_all x0 -> x1, blocking collectives: none -> 28.2 us  [shards(): lax.all_to_all(message, 'dev', split_axis=0, concat_axis=0, tiled=True)]
    convert_element_type x2 -> x0, local copies, waits for them, and re-layouts: 25.4 us -> none  [the longest x1 21.5 us: score_block(): features = jnp.einsum('bfu,fue->bfe', selector, feature_rows, preferred_e...]
    all_to_all x3 -> x1, starting transfers between devices: 29.4 us -> 7.73 us  [shards(): lax.all_to_all(pooled, 'dev', split_axis=0, concat_axis=0, tiled=True)]
  transfers between devices with their start and end apart: 3 -> 1, of which waited for: 3 -> 1; matrix products, arithmetic and copies ran while one was open for 2% -> 6% of each run, Pallas kernels for 0% -> 0%
where the time goes in v1:
time: 220 us; the launch traced here: 219 us
  Pallas kernels  113 us (51%)
  waiting for transfers between devices  50 us (23%)
  blocking collectives  28.2 us (13%)
  local copies, waits for them, and re-layouts  15.5 us (7%)
  starting transfers between devices  7.73 us (4%)
  other arithmetic  4.3 us (2%)
    pallas_call x1, Pallas kernels, pool_rows(): pl.pallas_call(functools.partial(pool_kernel, senders=senders, most_rows=...  78.7 us
    all_to_all x1, waiting for transfers between devices, shards(): lax.all_to_all(pooled, 'dev', split_axis=0, concat_axis=0, tiled=True)  50 us
    pallas_call x1, Pallas kernels, score_samples(): pl.pallas_call(tail_kernel, out_shape=jax.ShapeDtypeStruct((samples, unit...  34.4 us
    all_to_all x1, blocking collectives, shards(): lax.all_to_all(message, 'dev', split_axis=0, concat_axis=0, tiled=True)  28.2 us
    reshape x1, local copies, waits for them, and re-layouts, shards(): weight = jnp.transpose(top_weight.reshape(slots, mixes, -1), (1, 0, 2))  11.4 us
    all_to_all x1, starting transfers between devices, shards(): lax.all_to_all(pooled, 'dev', split_axis=0, concat_axis=0, tiled=True)  7.73 us
  transfers between devices with their start and end apart: 1, of which 1 were waited for; matrix products, arithmetic and copies ran while one was open for 6% of the time, Pallas kernels for 0%

profile of v1, /device:TPU:32, one launch (start us, length us, event | category | flops | bytes accessed | tf_op | source)
XLA Modules:
  0.0 219.1 jit_solution(8340674331984302501)
XLA Ops:
  0.0 0.0 copy-start
  0.0 0.5 broadcast.85
  0.5 1.5 reduce.3
  2.0 0.1 reshape_squeeze.6
  2.1 1.0 copy.36
  3.1 0.9 fusion.11
  4.0 0.1 copy.26
  4.2 0.1 reshape.66
  4.3 0.2 copy.27
  4.5 28.2 %all_to_all.16 = s32[128,1,384]{2,1,0:T(1,128)S(1)} all-to-all(s32[128,1,384]{2,1,0:T(1,128)S(1)} %copy.27), channel_id=1, replica_groups=mesh['dev'=128,'rep'=2] {'dev'}, dimensions={0} | all-to-all | bytes 393216 | tf_op jit(solution)/shard_map/all_to_all | solution.py:222
  32.7 0.0 copy-done
  32.8 78.7 %shard_map.91 = bf16[128,80,128]{2,1,0:T(8,128)(2,1)} custom-call(s32[128,384]{1,0:T(8,128)S(1)} %bitcast.74, bf16[8192,128]{1,0:T(8,128)(2,1)S(1)} %bitcast.75), custom_call_target="tpu_custom_call" | custom-call | flops 40000000000 | bytes 5242880 | tf_op jit(solution)/shard_map/pallas_call | solution.py:63
  111.5 0.0 copy-start.2
  111.5 7.7 %all-to-all-start.1 = ((bf16[128,80,128]{2,1,0:T(8,128)(2,1)}), bf16[128,80,128]{2,1,0:T(8,128)(2,1)S(1)}, u32[]{:S(2)}, u32[]{:S(2)}) async-start(bf16[128,80,128]{2,1,0:T(8,128)(2,1)} %shard_map.91), calls=%async_computation.1 | async-start | bytes 5242880 | tf_op jit(solution)/shard_map/all_to_all | solution.py:224
  119.2 0.2 reduce_window_sum.13
  119.4 0.1 add.80
  119.5 0.1 add.81
  119.6 0.1 reduce_window_sum.14
  119.7 0.0 copy-done.2
  119.7 0.1 copy.28
  119.9 0.0 copy-start.3
  119.9 0.0 copy-start.4
  119.9 11.4 %copy.35 = bf16[512,16,512]{2,0,1:T(8,128)(2,1)} copy(bf16[512,16,512]{2,1,0:T(8,128)(2,1)} %bitcast.76) | data formatting | bytes 16777216 | tf_op jit(solution)/shard_map/reshape | solution.py:237
  131.2 0.0 copy-done.3
  131.3 0.0 copy-done.4
  131.3 0.9 select_reduce_fusion
  132.1 0.9 fusion.1.pos_ref
  133.0 50.0 %all-to-all-done.1 = bf16[128,80,128]{2,1,0:T(8,128)(2,1)S(1)} async-done(((bf16[128,80,128]{2,1,0:T(8,128)(2,1)}), bf16[128,80,128]{2,1,0:T(8,128)(2,1)S(1)}, u32[]{:S(2)}, u32[]{:S(2)}) %all-to-all-start.1) | async-done | bytes 2621472 | tf_op jit(solution)/shard_map/all_to_all | solution.py:224
  183.0 0.0 copy-start.1
  183.0 1.6 copy-done.1
  184.5 34.4 %shard_map.92 = bf16[128,512]{1,0:T(8,128)(2,1)} custom-call(s32[512]{0:T(512)} %get-tuple-element.6.base_ref, bf16[10240,128]{1,0:T(8,128)(2,1)} %bitcast.78, bf16[512,128]{1,0:T(8,128)(2,1)} %fusion.1.pos_ref, bf16[16,512]{1,0:T(8,128)(2,1)} %compress_ref.1, bf16[16,512,512]{2,1,0:T(8,128)(2,1)} %bitcast.77, f32[1,512]{1,0:T(1,128)} %bitcast.82), custom_call_target="tpu_custom_call" | custom-call | flops 20000000000 | bytes 16777216 | tf_op jit(solution)/shard_map/pallas_call | solution.py:175
  (7 shorter events, 0.1 us)
Async XLA Ops:
  0.0 32.7 %copy-start = (bf16[4,2048,128]{2,1,0:T(8,128)(2,1)S(1)}, bf16[4,2048,128]{2,1,0:T(8,128)(2,1)}, u32[]{:S(2)}) copy-start(bf16[4,2048,128]{2,1,0:T(8,128)(2,1)} %param.9) | copy-start | bytes 6291460
  111.5 8.2 %copy-start.2 = (s32[128,512]{1,0:T(8,128)S(1)}, s32[128,512]{1,0:T(8,128)}, u32[]{:S(2)}) copy-start(s32[128,512]{1,0:T(8,128)} %param.13) | copy-start | bytes 786436
  111.5 71.5 %all-to-all-start.1 = ((bf16[128,80,128]{2,1,0:T(8,128)(2,1)}), bf16[128,80,128]{2,1,0:T(8,128)(2,1)S(1)}, u32[]{:S(2)}, u32[]{:S(2)}) async-start(bf16[128,80,128]{2,1,0:T(8,128)(2,1)} %shard_map.91), calls=%async_computation.1 | async-start | bytes 5242880 | tf_op jit(solution)/shard_map/all_to_all | solution.py:224
  119.9 11.4 %copy-start.3 = (s32[1,512]{1,0:T(1,128)S(1)}, s32[1,512]{1,0:T(1,128)}, u32[]{:S(2)}) copy-start(s32[1,512]{1,0:T(1,128)} %param.12) | copy-start | bytes 6148
  119.9 11.4 %copy-start.4 = (s32[512]{0:T(512)S(1)}, s32[512]{0:T(512)}, u32[]{:S(2)}) copy-start(s32[512]{0:T(512)} %param.14) | copy-start | bytes 6148
  183.0 1.6 copy-start.1

commit v2 on v1

v2 whole, which is shorter than its diff:
```python
import functools

import jax
import jax.numpy as jnp
from jax import lax
from jax.experimental import pallas as pl
from jax.experimental.pallas import tpu as pltpu
from jax.sharding import PartitionSpec as P

PACK_ROOM = 80
CHUNKS = ((0, 16), (16, 64))
BLOCK = 8
PARTS = 4
GROUP = 4


def message_kernel(ids_ref, lengths_ref, counts_ref, out_ref, words, *, vocabulary):
    most_rows, pool, slots = ids_ref.shape
    spare = GROUP * vocabulary
    slot = lax.broadcasted_iota(jnp.int32, (8, slots), 1) % GROUP
    counts = jnp.broadcast_to(counts_ref[...], (8, slots))
    offset = jnp.zeros((8, slots), jnp.int32)
    for back in range(1, GROUP):
        offset = offset + jnp.where(slot >= back, pltpu.roll(counts, back, 1), 0)
    offset = offset[:1, :]
    table = slot[:1, :] * vocabulary
    lengths = lengths_ref[...]
    used = lax.broadcasted_iota(jnp.int32, (most_rows, slots), 0) < counts[:1, :]
    room = 128
    for h in range(pool // 2):
        low = jnp.where(2 * h < lengths, ids_ref[:, 2 * h, :] + table, spare)
        high = jnp.where(2 * h + 1 < lengths, ids_ref[:, 2 * h + 1, :] + table, spare)
        word = jnp.where(used, low | (high << 16), 0)
        word = jnp.concatenate([word, jnp.zeros((8, slots), jnp.int32)], axis=0)
        for bit in range(3):
            moved = pltpu.roll(word, 1 << bit, 0)
            word = jnp.where(((offset >> bit) & 1) == 1, moved, word)
        word = jnp.concatenate(
            [word, jnp.zeros((room - word.shape[0], slots), jnp.int32)], axis=0
        )
        for bit in range(3, 7):
            by = 1 << bit
            moved = jnp.concatenate(
                [jnp.zeros((by, slots), jnp.int32), word[: room - by, :]], axis=0
            )
            word = jnp.where(((offset >> bit) & 1) == 1, moved, word)
        words[...] = jnp.transpose(word, (1, 0))
        groups = slots // GROUP
        total = words[pl.ds(0, groups, stride=GROUP), :]
        for member in range(1, GROUP):
            total = total + words[pl.ds(member, groups, stride=GROUP), :]
        out_ref[pl.ds(h, groups, stride=pool // 2), :] = total


def bag_message(bag_rows, bag_lengths, counts, vocabulary):
    slots, most_rows, pool = bag_rows.shape
    groups = slots // GROUP
    message = pl.pallas_call(
        functools.partial(message_kernel, vocabulary=vocabulary),
        out_shape=jax.ShapeDtypeStruct((groups * pool // 2, 128), jnp.int32),
        in_specs=[pl.BlockSpec(memory_space=pltpu.VMEM)] * 3,
        out_specs=pl.BlockSpec(memory_space=pltpu.VMEM),
        scratch_shapes=[pltpu.VMEM((slots, 128), jnp.int32)],
    )(jnp.transpose(bag_rows, (1, 2, 0)), jnp.transpose(bag_lengths, (1, 0)), counts)
    return message.reshape(groups, pool // 2, 128)


def pool_kernel(
    msg_ref, table_ref, out_ref, table_f32, pooled, ids, ids_smem, sems, *, first, rows, pool
):
    vocab_rows, emb = table_ref.shape
    peers = out_ref.shape[0]
    lanes = ids.shape[1]
    per = min(pool, lanes // rows)
    lines = pool // per
    shares = sems.shape[0]
    lane = lax.broadcasted_iota(jnp.int32, (peers, lanes), 1)
    held = []
    for h in range(pool // 2):
        word = msg_ref[pl.ds(h, peers, stride=pool // 2), :]
        held += [word & 0xFFFF, lax.shift_right_logical(word, 16)]
    for q in range(lines):
        line = jnp.zeros((peers, lanes), jnp.int32)
        for r in range(per):
            moved = pltpu.roll(held[q * per + r], (r * rows - first) % lanes, 1)
            line = jnp.where((lane >= r * rows) & (lane < (r + 1) * rows), moved, line)
        ids[pl.ds(q, peers, stride=lines), :] = line
    step = peers // shares
    copies = [
        pltpu.make_async_copy(
            ids.at[pl.ds(c * step * lines, step * lines)],
            ids_smem.at[pl.ds(c * step * lines, step * lines)],
            sems.at[c],
        )
        for c in range(shares)
    ]
    for copy in copies:
        copy.start()
    table_f32[pl.ds(vocab_rows, 8), :] = jnp.zeros((8, emb), jnp.float32)

    def widen(i, carry):
        at = pl.multiple_of(i * 256, 256)
        table_f32[pl.ds(at, 256), :] = table_ref[pl.ds(at, 256), :].astype(jnp.float32)
        return carry

    lax.fori_loop(0, vocab_rows // 256, widen, 0)

    def one_sender(d, carry):
        views = [ids_smem.at[pl.ds(d * lines + q, 1)] for q in range(lines)]
        for j in range(rows):
            parts = [
                table_f32[pl.ds(views[p // per][0, (p % per) * rows + j], 1), :]
                for p in range(pool)
            ]
            while len(parts) > 1:
                parts = [parts[i] + parts[i + 1] for i in range(0, len(parts), 2)]
            pooled[pl.ds(d * rows + j, 1), :] = parts[0]
        return carry

    for c in range(shares):
        copies[c].wait()
        lax.fori_loop(c * step, (c + 1) * step, one_sender, 0)

    def narrow(d, carry):
        at = pl.multiple_of(d * rows, 8)
        out_ref[d] = pooled[pl.ds(at, rows), :].astype(jnp.bfloat16)
        return carry

    lax.fori_loop(0, peers, narrow, 0, unroll=4)


def pool_rows(message, table_rows, first, rows):
    peers, halves, width = message.shape
    pool = 2 * halves
    lines = pool // min(pool, width // rows)
    emb = table_rows.shape[1]
    vmem = pl.BlockSpec(memory_space=pltpu.VMEM)
    return pl.pallas_call(
        functools.partial(pool_kernel, first=first, rows=rows, pool=pool),
        out_shape=jax.ShapeDtypeStruct((peers, rows, emb), jnp.bfloat16),
        in_specs=[vmem, vmem],
        out_specs=vmem,
        scratch_shapes=[
            pltpu.VMEM((table_rows.shape[0] + 8, emb), jnp.float32),
            pltpu.VMEM((peers * rows, emb), jnp.float32),
            pltpu.VMEM((peers * lines, width), jnp.int32),
            pltpu.SMEM((peers * lines, width), jnp.int32),
            pltpu.SemaphoreType.DMA((4,)),
        ],
        compiler_params=pltpu.CompilerParams(vmem_limit_bytes=24 << 20),
        cost_estimate=pl.CostEstimate(flops=20_000_000_000, bytes_accessed=5 << 20, transcendentals=0),
    )(message.reshape(peers * halves, width), table_rows)


def selector_kernel(pos_ref, out_ref):
    blocks, rows, lanes = out_ref.shape
    samples = rows // BLOCK
    lane = lax.broadcasted_iota(jnp.int32, (BLOCK, lanes), 1).astype(jnp.float32)

    def one_block(i, carry):
        pos = pos_ref[pl.ds(pl.multiple_of(i * BLOCK, BLOCK), BLOCK), :]
        for b in range(0, samples, 2):
            pair = [
                jnp.where(jnp.broadcast_to(pos[:, c : c + 1], (BLOCK, lanes)) == lane, 1.0, 0.0)
                for c in (b, b + 1)
            ]
            out_ref[i, pl.ds(b * BLOCK, 2 * BLOCK), :] = jnp.concatenate(pair, axis=0).astype(
                jnp.bfloat16
            )
        return carry

    lax.fori_loop(0, blocks, one_block, 0)


def build_selectors(pos):
    features, samples = pos.shape
    blocks = features // BLOCK
    some = 4
    return pl.pallas_call(
        selector_kernel,
        grid=(blocks // some,),
        out_shape=jax.ShapeDtypeStruct((blocks, samples * BLOCK, 128), jnp.bfloat16),
        in_specs=[pl.BlockSpec((some * BLOCK, samples), lambda i: (i, 0))],
        out_specs=pl.BlockSpec((some, samples * BLOCK, 128), lambda i: (i, 0, 0)),
        compiler_params=pltpu.CompilerParams(vmem_limit_bytes=8 << 20),
        cost_estimate=pl.CostEstimate(flops=10_000_000_000, bytes_accessed=16 << 20, transcendentals=0),
    )(pos)


def tail_kernel(base_ref, selector_ref, compress_ref, weight_ref, bias_ref, *refs, most_rows):
    row_refs = refs[: len(CHUNKS)]
    (
        out_ref, rows_f32, feats, pairs, select_vmem, weight_vmem, select_sem, weight_sem,
    ) = refs[len(CHUNKS) :]
    groups, _, emb = row_refs[0].shape
    total_rows = groups * PACK_ROOM
    samples, features, _ = feats.shape
    mixes = compress_ref.shape[0]
    blocks = features // BLOCK
    share = blocks // PARTS
    copies = [
        pltpu.make_async_copy(
            selector_ref.at[pl.ds(part * share, share)],
            select_vmem.at[pl.ds(part * share, share)],
            select_sem.at[part],
        )
        for part in range(PARTS)
    ]
    for copy in copies:
        copy.start()
    weight_copy = pltpu.make_async_copy(weight_ref, weight_vmem, weight_sem)
    weight_copy.start()

    rows_f32[pl.ds(total_rows, most_rows), :] = jnp.zeros((most_rows, emb), jnp.float32)

    def widen(g, carry):
        for (first, count), row_ref in zip(CHUNKS, row_refs):
            at = pl.multiple_of(g * PACK_ROOM + first, 16)
            rows_f32[pl.ds(at, count), :] = row_ref[g].astype(jnp.float32)
        return carry

    lax.fori_loop(0, groups, widen, 0, unroll=4)

    first_half = lax.broadcasted_iota(jnp.int32, (1, BLOCK, emb), 1) < BLOCK // 2
    some = 32

    def expand(i, carry):
        for pair in range(2):
            tops = []
            for half in range(2):
                block = 4 * i + 2 * pair + half
                sides = []
                for side in range(2):
                    parts = []
                    for j in range(BLOCK // 2):
                        base = base_ref[block * BLOCK + side * (BLOCK // 2) + j]
                        parts.append(rows_f32[pl.ds(base, most_rows), :].astype(jnp.bfloat16))
                    sides.append(jnp.concatenate(parts, axis=0))
                tops.append((block, jnp.concatenate(sides, axis=1)))
            at = pl.multiple_of((4 * i + 2 * pair) * BLOCK, 2 * BLOCK)
            for c in range(samples // some):
                halves = []
                for block, rhs in tops:
                    lhs = select_vmem[block, pl.ds(c * some * BLOCK, some * BLOCK), :]
                    got = jnp.dot(lhs, rhs, preferred_element_type=jnp.float32)
                    got = got.reshape(some, BLOCK, 2 * emb)
                    halves.append(jnp.where(first_half, got[:, :, :emb], got[:, :, emb:]))
                both = jnp.concatenate(halves, axis=1)
                feats[pl.ds(c * some, some), pl.ds(at, 2 * BLOCK), :] = both.astype(jnp.bfloat16)
        return carry

    for part in range(PARTS):
        copies[part].wait()
        lax.fori_loop(part * share // 4, (part + 1) * share // 4, expand, 0)

    per = 8

    def score(i, carry):
        mixing = compress_ref[...]
        stacks = []
        mixed = []
        for j in range(per // 2):
            b = i * per + 2 * j
            both = jnp.concatenate([feats[b], feats[b + 1]], axis=1)
            stacks.append(both)
            mixed.append(
                jnp.dot(mixing, both, preferred_element_type=jnp.float32).astype(jnp.bfloat16)
            )
        for j in range(per // 2):
            none = jnp.zeros((mixes, emb), jnp.bfloat16)
            first = jnp.concatenate([mixed[j][:, :emb], none], axis=1)
            second = jnp.concatenate([none, mixed[j][:, emb:]], axis=1)
            lhs = jnp.concatenate([first, second], axis=0)
            got = jnp.dot(lhs, jnp.transpose(stacks[j]), preferred_element_type=jnp.float32)
            at = pl.multiple_of((i * per + 2 * j) * mixes, 2 * mixes)
            for c in range(features // 128):
                pairs[c, pl.ds(at, 2 * mixes), :] = got[:, c * 128 : (c + 1) * 128]
        return carry

    lax.fori_loop(0, samples // per, score, 0)

    weight_copy.wait()
    total = jnp.broadcast_to(bias_ref[...], (samples, out_ref.shape[1]))
    for k in range(mixes):
        lhs = jnp.concatenate(
            [pairs[c, pl.ds(k, samples, stride=mixes), :] for c in range(features // 128)], axis=1
        ).astype(jnp.bfloat16)
        total = total + jnp.dot(lhs, weight_vmem[k], preferred_element_type=jnp.float32)
    out_ref[...] = jnp.maximum(total, 0.0).astype(jnp.bfloat16)


def score_samples(base, selectors, arrived, compress, weight, bias, most_rows):
    mixes, features = compress.shape
    units = weight.shape[2]
    groups, _, emb = arrived[0].shape
    samples = selectors.shape[1] // BLOCK
    vmem = pl.BlockSpec(memory_space=pltpu.VMEM)
    hbm = pl.BlockSpec(memory_space=pltpu.HBM)
    return pl.pallas_call(
        functools.partial(tail_kernel, most_rows=most_rows),
        out_shape=jax.ShapeDtypeStruct((samples, units), jnp.bfloat16),
        in_specs=[pl.BlockSpec(memory_space=pltpu.SMEM), hbm, vmem, hbm, vmem]
        + [vmem] * len(arrived),
        out_specs=vmem,
        scratch_shapes=[
            pltpu.VMEM((groups * PACK_ROOM + most_rows, emb), jnp.float32),
            pltpu.VMEM((samples, features, emb), jnp.bfloat16),
            pltpu.VMEM((features // 128, samples * mixes, 128), jnp.float32),
            pltpu.VMEM(selectors.shape, jnp.bfloat16),
            pltpu.VMEM(weight.shape, jnp.bfloat16),
            pltpu.SemaphoreType.DMA((PARTS,)),
            pltpu.SemaphoreType.DMA(()),
        ],
        compiler_params=pltpu.CompilerParams(vmem_limit_bytes=53 << 20),
        cost_estimate=pl.CostEstimate(flops=20_000_000_000, bytes_accessed=16 << 20, transcendentals=0),
    )(base, selectors, compress, weight, bias, *arrived)


def shards(
    tables, bag_rows, bag_lengths, row_counts, inverse, table_order, compress, top_weight, top_bias
):
    vocabulary, emb = tables.shape[1:]
    slots = table_order.shape[0]
    most_rows = bag_rows.shape[2]
    mixes = compress.shape[0]
    counts = row_counts[0]
    message = bag_message(bag_rows[0], bag_lengths[0], row_counts, vocabulary)
    got = lax.all_to_all(message, "dev", split_axis=0, concat_axis=0, tiled=True)
    table_rows = tables.reshape(-1, emb)
    arrived = []
    for first, count in CHUNKS:
        pooled = pool_rows(got, table_rows, first, count)
        arrived.append(lax.all_to_all(pooled, "dev", split_axis=0, concat_axis=0, tiled=True))

    grouped = counts.reshape(-1, GROUP)
    before = jnp.cumsum(grouped, axis=1) - grouped
    group_at = jnp.arange(slots // GROUP, dtype=jnp.int32)[:, None] * PACK_ROOM
    slot_base = (before + group_at).reshape(-1)
    slot_range = jnp.arange(slots, dtype=jnp.int32)
    matches = table_order[:, None] == slot_range[None, :]
    feature_base = jnp.sum(jnp.where(matches, slot_base[:, None], 0), axis=0)
    feature_count = jnp.sum(jnp.where(matches, counts[:, None], 0), axis=0)
    shift = (slot_range % (BLOCK // 2)) * most_rows
    pos = jnp.where(inverse < feature_count[None, :], inverse + shift[None, :], -1)
    selectors = build_selectors(jnp.transpose(pos.astype(jnp.float32), (1, 0)))
    weight = jnp.transpose(top_weight.reshape(slots, mixes, -1), (1, 0, 2))
    return score_samples(
        feature_base, selectors, arrived, compress, weight, top_bias[None, :], most_rows
    )


def solution(mesh):
    return jax.shard_map(
        shards,
        mesh=mesh,
        in_specs=(
            P("dev", None, None),
            P(("rep", "dev"), None, None, None),
            P(("rep", "dev"), None, None),
            P(("rep", "dev"), None),
            P(("rep", "dev"), None),
            P(),
            P(),
            P(),
            P(),
        ),
        out_specs=P(("rep", "dev"), None),
        check_vma=False,
    )
```

time: 220 us -> 167 us (0.76)
  waiting for transfers between devices: 50 us -> 13.3 us
  Pallas kernels: 113 us -> 82.7 us
  starting transfers between devices: 7.73 us -> 20.3 us
  local copies, waits for them, and re-layouts: 15.5 us -> 21.1 us
  other arithmetic: 4.3 us -> 1.34 us
    all_to_all x1 -> x2, waiting for transfers between devices: 50 us -> 13.3 us  [shards(): lax.all_to_all(pooled, 'dev', split_axis=0, concat_axis=0, tiled=True)]
    pallas_call x2 -> x5, Pallas kernels: 113 us -> 82.7 us  [the longest x2 34.7 us: pool_rows(): pl.pallas_call(functools.partial(pool_kernel, first=first, rows=rows, poo...]
    all_to_all x1 -> x2, starting transfers between devices: 7.73 us -> 20.3 us  [shards(): lax.all_to_all(pooled, 'dev', split_axis=0, concat_axis=0, tiled=True)]
    unnamed x14 -> x20, local copies, waits for them, and re-layouts: 3.28 us -> 9.35 us
  transfers between devices with their start and end apart: 1 -> 2, of which waited for: 1 -> 1; matrix products, arithmetic and copies ran while one was open for 6% -> 8% of each run, Pallas kernels for 0% -> 27%
where the time goes in v2:
time: 167 us; the launch traced here: 166 us
  Pallas kernels  82.7 us (50%)
  blocking collectives  27.1 us (16%)
  local copies, waits for them, and re-layouts  21.1 us (13%)
  starting transfers between devices  20.3 us (12%)
  waiting for transfers between devices  13.3 us (8%)
    pallas_call x2, Pallas kernels, pool_rows(): pl.pallas_call(functools.partial(pool_kernel, first=first, rows=rows, poo...  34.7 us
    pallas_call x1, Pallas kernels, score_samples(): pl.pallas_call(functools.partial(tail_kernel, most_rows=most_rows), out_s...  27.2 us
    all_to_all x1, blocking collectives, shards(): lax.all_to_all(message, 'dev', split_axis=0, concat_axis=0, tiled=True)  27.1 us
    all_to_all x2, starting transfers between devices, shards(): lax.all_to_all(pooled, 'dev', split_axis=0, concat_axis=0, tiled=True)  20.3 us
    pallas_call x1, Pallas kernels, build_selectors(): pl.pallas_call(selector_kernel, grid=(blocks // some,), out_shape=jax.Sha...  18.8 us
    all_to_all x2, waiting for transfers between devices, shards(): lax.all_to_all(pooled, 'dev', split_axis=0, concat_axis=0, tiled=True)  13.3 us
    reshape x1, local copies, waits for them, and re-layouts, shards(): weight = jnp.transpose(top_weight.reshape(slots, mixes, -1), (1, 0, 2))  11.3 us
    unnamed x20, local copies, waits for them, and re-layouts  9.35 us
  transfers between devices with their start and end apart: 2, of which 1 were waited for; matrix products, arithmetic and copies ran while one was open for 8% of the time, Pallas kernels for 27%

profile of v2, /device:TPU:32, one launch (start us, length us, event | category | flops | bytes accessed | tf_op | source)
XLA Modules:
  0.0 166.2 jit_solution(3372042963079983563)
XLA Ops:
  0.0 2.0 %shard_map.92 = s32[256,128]{1,0:T(8,128)} custom-call(s32[32,4,512]{2,1,0:T(4,128)} %bitcast.25, s32[32,512]{1,0:T(8,128)} %bitcast.26, s32[1,512]{1,0:T(1,128)} %counts_ref.1), custom_call_target="tpu_custom_call" | custom-call | tf_op jit(solution)/shard_map/pallas_call | solution.py:58
  2.0 27.1 %all_to_all.15 = s32[128,2,128]{2,1,0:T(2,128)S(1)} all-to-all(s32[128,2,128]{2,1,0:T(2,128)} %bitcast.24), channel_id=1, replica_groups=mesh['dev'=128,'rep'=2] {'dev'}, dimensions={0} | all-to-all | bytes 262144 | tf_op jit(solution)/shard_map/all_to_all | solution.py:328
  29.1 0.0 copy-start
  29.1 1.6 copy-done
  30.7 0.0 copy-start.1
  30.7 9.3 %shard_map.93 = bf16[128,16,128]{2,1,0:T(8,128)(2,1)} custom-call(s32[256,128]{1,0:T(8,128)S(1)} %bitcast.17, bf16[8192,128]{1,0:T(8,128)(2,1)S(1)} %bitcast.19), custom_call_target="tpu_custom_call" | custom-call | flops 20000000000 | bytes 5242880 | tf_op jit(solution)/shard_map/pallas_call | solution.py:138
  40.0 6.5 %all-to-all-start.1 = ((bf16[128,16,128]{2,1,0:T(8,128)(2,1)}), bf16[128,16,128]{2,1,0:T(8,128)(2,1)S(1)}, u32[]{:S(2)}, u32[]{:S(2)}) async-start(bf16[128,16,128]{2,1,0:T(8,128)(2,1)} %shard_map.93), calls=%async_computation.1 | async-start | bytes 1048576 | tf_op jit(solution)/shard_map/all_to_all | solution.py:333
  46.5 0.0 copy-done.1
  46.5 0.0 copy-start.7
  46.5 0.0 copy-start.6
  46.5 25.4 %shard_map.94 = bf16[128,64,128]{2,1,0:T(8,128)(2,1)} custom-call(s32[256,128]{1,0:T(8,128)S(1)} %bitcast.18, bf16[8192,128]{1,0:T(8,128)(2,1)S(1)} %bitcast.20), custom_call_target="tpu_custom_call" | custom-call | flops 20000000000 | bytes 5242880 | tf_op jit(solution)/shard_map/pallas_call | solution.py:138
  71.9 0.0 all-to-all-done.1.refs_0_
  71.9 13.8 %all-to-all-start.2 = ((bf16[128,64,128]{2,1,0:T(8,128)(2,1)}), bf16[128,64,128]{2,1,0:T(8,128)(2,1)S(1)}, u32[]{:S(2)}, u32[]{:S(2)}) async-start(bf16[128,64,128]{2,1,0:T(8,128)(2,1)} %shard_map.94), calls=%async_computation.2 | async-start | bytes 4194304 | tf_op jit(solution)/shard_map/all_to_all | solution.py:333
  85.7 0.5 broadcast.37
  86.2 0.0 copy-done.7
  86.2 0.7 reduce.3
  86.9 0.1 reshape_squeeze.5
  87.0 0.2 reduce_window_sum.13
  87.2 0.1 reduce_window_sum.14
  87.3 0.1 add.32
  87.4 0.1 add.33
  87.5 0.0 copy-done.6
  87.5 0.1 copy.15
  87.6 0.0 copy-start.8
  87.7 11.3 %copy.19 = bf16[512,16,512]{2,0,1:T(8,128)(2,1)} copy(bf16[512,16,512]{2,1,0:T(8,128)(2,1)} %bitcast.22) | data formatting | bytes 16777216 | tf_op jit(solution)/shard_map/reshape | solution.py:346
  99.0 0.0 copy-done.8
  99.0 0.3 select_reduce_fusion
  99.3 0.2 convert_bitcast_fusion.pos_ref
  99.5 0.0 copy-start.2
  99.5 0.0 copy-start.3
  99.5 18.8 %shard_map.91.selector_ref = bf16[64,1024,128]{2,1,0:T(8,128)(2,1)S(1)} custom-call(f32[512,128]{1,0:T(8,128)S(1)} %convert_bitcast_fusion.pos_ref), custom_call_target="tpu_custom_call" | custom-call | flops 10000000000 | bytes 16777216 | tf_op jit(solution)/shard_map/pallas_call | solution.py:179
  118.4 0.0 copy-start.4
  118.4 5.7 %copy-done.4 = bf16[64,1024,128]{2,1,0:T(8,128)(2,1)} copy-done((bf16[64,1024,128]{2,1,0:T(8,128)(2,1)}, bf16[64,1024,128]{2,1,0:T(8,128)(2,1)S(1)}, u32[]{:S(2)}) %copy-start.4) | copy-done | bytes 16777240
  124.1 13.3 %all-to-all-done.2.refs_1_ = bf16[128,64,128]{2,1,0:T(8,128)(2,1)S(1)} async-done(((bf16[128,64,128]{2,1,0:T(8,128)(2,1)}), bf16[128,64,128]{2,1,0:T(8,128)(2,1)S(1)}, u32[]{:S(2)}, u32[]{:S(2)}) %all-to-all-start.2) | async-done | bytes 2097184 | tf_op jit(solution)/shard_map/all_to_all | solution.py:333
  137.5 0.0 copy-start.5
  137.5 1.4 copy-done.5
  138.8 0.0 copy-done.2
  138.8 0.0 copy-done.3
  138.8 27.2 %shard_map.95 = bf16[128,512]{1,0:T(8,128)(2,1)} custom-call(s32[512]{0:T(512)S(1)} %get-tuple-element.6.base_ref, bf16[64,1024,128]{2,1,0:T(8,128)(2,1)} %copy-done.4, bf16[16,512]{1,0:T(8,128)(2,1)S(1)} %copy-done.2, bf16[16,512,512]{2,1,0:T(8,128)(2,1)} %bitcast.23, f32[1,512]{1,0:T(1,128)S(1)} %bitcast.21, ...), custom_call_target="tpu_custom_call" | custom-call | flops 20000000000 | bytes 16777216 | tf_op jit(solution)/shard_map/pallas_call | solution.py:299
  (3 shorter events, 0.0 us)
Async XLA Ops:
  29.1 1.6 copy-start
  30.7 15.8 %copy-start.1 = (bf16[4,2048,128]{2,1,0:T(8,128)(2,1)S(1)}, bf16[4,2048,128]{2,1,0:T(8,128)(2,1)}, u32[]{:S(2)}) copy-start(bf16[4,2048,128]{2,1,0:T(8,128)(2,1)} %param.9) | copy-start | bytes 6291460
  40.0 31.9 %all-to-all-start.1 = ((bf16[128,16,128]{2,1,0:T(8,128)(2,1)}), bf16[128,16,128]{2,1,0:T(8,128)(2,1)S(1)}, u32[]{:S(2)}, u32[]{:S(2)}) async-start(bf16[128,16,128]{2,1,0:T(8,128)(2,1)} %shard_map.93), calls=%async_computation.1 | async-start | bytes 1048576 | tf_op jit(solution)/shard_map/all_to_all | solution.py:333
  46.5 39.7 %copy-start.7 = (s32[1,512]{1,0:T(1,128)S(1)}, s32[1,512]{1,0:T(1,128)}, u32[]{:S(2)}) copy-start(s32[1,512]{1,0:T(1,128)} %counts_ref.1) | copy-start | bytes 6148
  46.5 41.0 %copy-start.6 = (s32[128,512]{1,0:T(8,128)S(1)}, s32[128,512]{1,0:T(8,128)}, u32[]{:S(2)}) copy-start(s32[128,512]{1,0:T(8,128)} %param.13) | copy-start | bytes 786436
  71.9 65.5 %all-to-all-start.2 = ((bf16[128,64,128]{2,1,0:T(8,128)(2,1)}), bf16[128,64,128]{2,1,0:T(8,128)(2,1)S(1)}, u32[]{:S(2)}, u32[]{:S(2)}) async-start(bf16[128,64,128]{2,1,0:T(8,128)(2,1)} %shard_map.94), calls=%async_computation.2 | async-start | bytes 4194304 | tf_op jit(solution)/shard_map/all_to_all | solution.py:333
  87.6 11.4 %copy-start.8 = (s32[512]{0:T(512)S(1)}, s32[512]{0:T(512)}, u32[]{:S(2)}) copy-start(s32[512]{0:T(512)} %param.14) | copy-start | bytes 6148
  99.5 39.3 %copy-start.2 = (bf16[16,512]{1,0:T(8,128)(2,1)S(1)}, bf16[16,512]{1,0:T(8,128)(2,1)}, u32[]{:S(2)}) copy-start(bf16[16,512]{1,0:T(8,128)(2,1)} %compress_ref.1) | copy-start | bytes 49156
  99.5 39.3 %copy-start.3 = (f32[512]{0:T(512)S(1)}, f32[512]{0:T(512)}, u32[]{:S(2)}) copy-start(f32[512]{0:T(512)} %param.17) | copy-start | bytes 6148
  118.4 5.7 %copy-start.4 = (bf16[64,1024,128]{2,1,0:T(8,128)(2,1)}, bf16[64,1024,128]{2,1,0:T(8,128)(2,1)S(1)}, u32[]{:S(2)}) copy-start(bf16[64,1024,128]{2,1,0:T(8,128)(2,1)S(1)} %shard_map.91.selector_ref) | copy-start | bytes 50331652
  137.5 1.4 copy-start.5

commit v3 on v2

--- a/solution.py
+++ b/solution.py
@@ -8,7 +8,7 @@
 from jax.sharding import PartitionSpec as P
 
 PACK_ROOM = 80
-CHUNKS = ((0, 16), (16, 64))
+CHUNKS = ((0, 80),)
 BLOCK = 8
 PARTS = 4
 GROUP = 4
@@ -66,13 +66,16 @@
 
 
 def pool_kernel(
-    msg_ref, table_ref, out_ref, table_f32, pooled, ids, ids_smem, sems, *, first, rows, pool
+    msg_ref, table_hbm, out_ref, table_ref, table_f32, pooled, ids, ids_smem, sems, table_sem,
+    *, first, rows, pool,
 ):
-    vocab_rows, emb = table_ref.shape
+    vocab_rows, emb = table_hbm.shape
+    table_copy = pltpu.make_async_copy(table_hbm, table_ref, table_sem)
+    table_copy.start()
     peers = out_ref.shape[0]
     lanes = ids.shape[1]
     per = min(pool, lanes // rows)
-    lines = pool // per
+    lines = -(-pool // per)
     shares = sems.shape[0]
     lane = lax.broadcasted_iota(jnp.int32, (peers, lanes), 1)
     held = []
@@ -97,6 +100,7 @@
     for copy in copies:
         copy.start()
     table_f32[pl.ds(vocab_rows, 8), :] = jnp.zeros((8, emb), jnp.float32)
+    table_copy.wait()
 
     def widen(i, carry):
         at = pl.multiple_of(i * 256, 256)
@@ -132,20 +136,22 @@
 def pool_rows(message, table_rows, first, rows):
     peers, halves, width = message.shape
     pool = 2 * halves
-    lines = pool // min(pool, width // rows)
+    lines = -(-pool // min(pool, width // rows))
     emb = table_rows.shape[1]
     vmem = pl.BlockSpec(memory_space=pltpu.VMEM)
     return pl.pallas_call(
         functools.partial(pool_kernel, first=first, rows=rows, pool=pool),
         out_shape=jax.ShapeDtypeStruct((peers, rows, emb), jnp.bfloat16),
-        in_specs=[vmem, vmem],
+        in_specs=[vmem, pl.BlockSpec(memory_space=pltpu.HBM)],
         out_specs=vmem,
         scratch_shapes=[
+            pltpu.VMEM(table_rows.shape, jnp.bfloat16),
             pltpu.VMEM((table_rows.shape[0] + 8, emb), jnp.float32),
             pltpu.VMEM((peers * rows, emb), jnp.float32),
             pltpu.VMEM((peers * lines, width), jnp.int32),
             pltpu.SMEM((peers * lines, width), jnp.int32),
             pltpu.SemaphoreType.DMA((4,)),
+            pltpu.SemaphoreType.DMA(()),
         ],
         compiler_params=pltpu.CompilerParams(vmem_limit_bytes=24 << 20),
         cost_estimate=pl.CostEstimate(flops=20_000_000_000, bytes_accessed=5 << 20, transcendentals=0),
@@ -154,19 +160,28 @@
 
 def selector_kernel(pos_ref, out_ref):
     blocks, rows, lanes = out_ref.shape
-    samples = rows // BLOCK
-    lane = lax.broadcasted_iota(jnp.int32, (BLOCK, lanes), 1).astype(jnp.float32)
+    pairs = rows // BLOCK
+    half = lanes // 2
+    lane = lax.broadcasted_iota(jnp.int32, (BLOCK, half), 1).astype(jnp.float32)
+    upper = lax.broadcasted_iota(jnp.int32, (BLOCK, pos_ref.shape[1]), 0) < BLOCK // 2
 
     def one_block(i, carry):
-        pos = pos_ref[pl.ds(pl.multiple_of(i * BLOCK, BLOCK), BLOCK), :]
-        for b in range(0, samples, 2):
-            pair = [
-                jnp.where(jnp.broadcast_to(pos[:, c : c + 1], (BLOCK, lanes)) == lane, 1.0, 0.0)
-                for c in (b, b + 1)
-            ]
-            out_ref[i, pl.ds(b * BLOCK, 2 * BLOCK), :] = jnp.concatenate(pair, axis=0).astype(
-                jnp.bfloat16
-            )
+        here = pos_ref[pl.ds(pl.multiple_of(i * BLOCK, BLOCK), BLOCK), :]
+        swapped = pltpu.roll(here, BLOCK // 2, 0)
+        samples = here.shape[1]
+        sides = (
+            jnp.where(upper, here, pltpu.roll(swapped, samples - 1, 1)),
+            jnp.where(upper, swapped, pltpu.roll(here, samples - 1, 1)),
+        )
+        for side, pos in enumerate(sides):
+            for p in range(0, pairs, 2):
+                both = [
+                    jnp.where(jnp.broadcast_to(pos[:, c : c + 1], (BLOCK, half)) == lane, 1.0, 0.0)
+                    for c in (2 * p, 2 * p + 2)
+                ]
+                out_ref[i, pl.ds(p * BLOCK, 2 * BLOCK), pl.ds(side * half, half)] = (
+                    jnp.concatenate(both, axis=0).astype(jnp.bfloat16)
+                )
         return carry
 
     lax.fori_loop(0, blocks, one_block, 0)
@@ -175,13 +190,14 @@
 def build_selectors(pos):
     features, samples = pos.shape
     blocks = features // BLOCK
+    pairs = samples // 2
     some = 4
     return pl.pallas_call(
         selector_kernel,
         grid=(blocks // some,),
-        out_shape=jax.ShapeDtypeStruct((blocks, samples * BLOCK, 128), jnp.bfloat16),
+        out_shape=jax.ShapeDtypeStruct((blocks, pairs * BLOCK, 256), jnp.bfloat16),
         in_specs=[pl.BlockSpec((some * BLOCK, samples), lambda i: (i, 0))],
-        out_specs=pl.BlockSpec((some, samples * BLOCK, 128), lambda i: (i, 0, 0)),
+        out_specs=pl.BlockSpec((some, pairs * BLOCK, 256), lambda i: (i, 0, 0)),
         compiler_params=pltpu.CompilerParams(vmem_limit_bytes=8 << 20),
         cost_estimate=pl.CostEstimate(flops=10_000_000_000, bytes_accessed=16 << 20, transcendentals=0),
     )(pos)
@@ -190,11 +206,12 @@
 def tail_kernel(base_ref, selector_ref, compress_ref, weight_ref, bias_ref, *refs, most_rows):
     row_refs = refs[: len(CHUNKS)]
     (
-        out_ref, rows_f32, feats, pairs, select_vmem, weight_vmem, select_sem, weight_sem,
+        out_ref, rows_f32, feats, pairs, turned, select_vmem, weight_vmem, select_sem, weight_sem,
     ) = refs[len(CHUNKS) :]
     groups, _, emb = row_refs[0].shape
     total_rows = groups * PACK_ROOM
-    samples, features, _ = feats.shape
+    sample_pairs, _, features, _ = feats.shape
+    samples = 2 * sample_pairs
     mixes = compress_ref.shape[0]
     blocks = features // BLOCK
     share = blocks // PARTS
@@ -223,6 +240,7 @@
 
     first_half = lax.broadcasted_iota(jnp.int32, (1, BLOCK, emb), 1) < BLOCK // 2
     some = 32
+    empty = jnp.zeros((BLOCK // 2 * most_rows, emb), jnp.bfloat16)
 
     def expand(i, carry):
         for pair in range(2):
@@ -236,17 +254,23 @@
                         base = base_ref[block * BLOCK + side * (BLOCK // 2) + j]
                         parts.append(rows_f32[pl.ds(base, most_rows), :].astype(jnp.bfloat16))
                     sides.append(jnp.concatenate(parts, axis=0))
-                tops.append((block, jnp.concatenate(sides, axis=1)))
+                top = jnp.concatenate([sides[0], empty], axis=1)
+                bottom = jnp.concatenate([empty, sides[1]], axis=1)
+                tops.append((block, jnp.concatenate([top, bottom], axis=0)))
             at = pl.multiple_of((4 * i + 2 * pair) * BLOCK, 2 * BLOCK)
-            for c in range(samples // some):
-                halves = []
+            for c in range(sample_pairs // some):
+                even, odd = [], []
                 for block, rhs in tops:
                     lhs = select_vmem[block, pl.ds(c * some * BLOCK, some * BLOCK), :]
                     got = jnp.dot(lhs, rhs, preferred_element_type=jnp.float32)
                     got = got.reshape(some, BLOCK, 2 * emb)
-                    halves.append(jnp.where(first_half, got[:, :, :emb], got[:, :, emb:]))
-                both = jnp.concatenate(halves, axis=1)
-                feats[pl.ds(c * some, some), pl.ds(at, 2 * BLOCK), :] = both.astype(jnp.bfloat16)
+                    left, right = got[:, :, :emb], got[:, :, emb:]
+                    even.append(jnp.where(first_half, left, pltpu.roll(right, BLOCK // 2, 1)))
+                    odd.append(jnp.where(first_half, pltpu.roll(left, BLOCK // 2, 1), right))
+                for which, parts in enumerate((even, odd)):
+                    feats[pl.ds(c * some, some), which, pl.ds(at, 2 * BLOCK), :] = jnp.concatenate(
+                        parts, axis=1
+                    ).astype(jnp.bfloat16)
         return carry
 
     for part in range(PARTS):
@@ -257,12 +281,11 @@
 
     def score(i, carry):
         mixing = compress_ref[...]
-        stacks = []
         mixed = []
         for j in range(per // 2):
-            b = i * per + 2 * j
-            both = jnp.concatenate([feats[b], feats[b + 1]], axis=1)
-            stacks.append(both)
+            at = i * (per // 2) + j
+            both = jnp.concatenate([feats[at, 0], feats[at, 1]], axis=1)
+            turned[j] = jnp.transpose(both)
             mixed.append(
                 jnp.dot(mixing, both, preferred_element_type=jnp.float32).astype(jnp.bfloat16)
             )
@@ -271,7 +294,7 @@
             first = jnp.concatenate([mixed[j][:, :emb], none], axis=1)
             second = jnp.concatenate([none, mixed[j][:, emb:]], axis=1)
             lhs = jnp.concatenate([first, second], axis=0)
-            got = jnp.dot(lhs, jnp.transpose(stacks[j]), preferred_element_type=jnp.float32)
+            got = jnp.dot(lhs, turned[j], preferred_element_type=jnp.float32)
             at = pl.multiple_of((i * per + 2 * j) * mixes, 2 * mixes)
             for c in range(features // 128):
                 pairs[c, pl.ds(at, 2 * mixes), :] = got[:, c * 128 : (c + 1) * 128]
@@ -293,7 +316,7 @@
     mixes, features = compress.shape
     units = weight.shape[2]
     groups, _, emb = arrived[0].shape
-    samples = selectors.shape[1] // BLOCK
+    samples = 2 * selectors.shape[1] // BLOCK
     vmem = pl.BlockSpec(memory_space=pltpu.VMEM)
     hbm = pl.BlockSpec(memory_space=pltpu.HBM)
     return pl.pallas_call(
@@ -304,8 +327,9 @@
         out_specs=vmem,
         scratch_shapes=[
             pltpu.VMEM((groups * PACK_ROOM + most_rows, emb), jnp.float32),
-            pltpu.VMEM((samples, features, emb), jnp.bfloat16),
+            pltpu.VMEM((samples // 2, 2, features, emb), jnp.bfloat16),
             pltpu.VMEM((features // 128, samples * mixes, 128), jnp.float32),
+            pltpu.VMEM((4, 2 * emb, features), jnp.bfloat16),
             pltpu.VMEM(selectors.shape, jnp.bfloat16),
             pltpu.VMEM(weight.shape, jnp.bfloat16),
             pltpu.SemaphoreType.DMA((PARTS,)),

time: 167 us -> 154 us (0.922)
  starting transfers between devices: 20.3 us -> 6.54 us
  waiting for transfers between devices: 13.3 us -> 20 us
  Pallas kernels: 82.7 us -> 76.7 us
    all_to_all x2 -> x1, starting transfers between devices: 20.3 us -> 6.54 us  [shards(): lax.all_to_all(pooled, 'dev', split_axis=0, concat_axis=0, tiled=True)]
    all_to_all x2 -> x1, waiting for transfers between devices: 13.3 us -> 20 us  [shards(): lax.all_to_all(pooled, 'dev', split_axis=0, concat_axis=0, tiled=True)]
    pallas_call x2 -> x1, Pallas kernels: 34.7 us -> 29.1 us  [pool_rows(): pl.pallas_call(functools.partial(pool_kernel, first=first, rows=rows, poo...]
    pallas_call x1, Pallas kernels: 27.2 us -> 22.1 us  [score_samples(): pl.pallas_call(functools.partial(tail_kernel, most_rows=most_rows), out_s...]
    pallas_call x1, Pallas kernels: 18.8 us -> 23.5 us  [build_selectors(): pl.pallas_call(selector_kernel, grid=(blocks // some,), out_shape=jax.Sha...]
    unnamed x20 -> x18, local copies, waits for them, and re-layouts: 9.35 us -> 9.53 us
  transfers between devices with their start and end apart: 2 -> 1, of which waited for: 1 -> 1; matrix products, arithmetic and copies ran while one was open for 8% -> 9% of each run, Pallas kernels for 27% -> 15%
where the time goes in v3:
time: 154 us; the launch traced here: 153 us
  Pallas kernels  76.7 us (50%)
  blocking collectives  27.1 us (18%)
  local copies, waits for them, and re-layouts  21.3 us (14%)
  waiting for transfers between devices  20 us (13%)
  starting transfers between devices  6.54 us (4%)
    pallas_call x1, Pallas kernels, pool_rows(): pl.pallas_call(functools.partial(pool_kernel, first=first, rows=rows, poo...  29.1 us
    all_to_all x1, blocking collectives, shards(): lax.all_to_all(message, 'dev', split_axis=0, concat_axis=0, tiled=True)  27.1 us
    pallas_call x1, Pallas kernels, build_selectors(): pl.pallas_call(selector_kernel, grid=(blocks // some,), out_shape=jax.Sha...  23.5 us
    pallas_call x1, Pallas kernels, score_samples(): pl.pallas_call(functools.partial(tail_kernel, most_rows=most_rows), out_s...  22.1 us
    all_to_all x1, waiting for transfers between devices, shards(): lax.all_to_all(pooled, 'dev', split_axis=0, concat_axis=0, tiled=True)  20 us
    reshape x1, local copies, waits for them, and re-layouts, shards(): weight = jnp.transpose(top_weight.reshape(slots, mixes, -1), (1, 0, 2))  11.3 us
    unnamed x18, local copies, waits for them, and re-layouts  9.53 us
    all_to_all x1, starting transfers between devices, shards(): lax.all_to_all(pooled, 'dev', split_axis=0, concat_axis=0, tiled=True)  6.54 us
  transfers between devices with their start and end apart: 1, of which 1 were waited for; matrix products, arithmetic and copies ran while one was open for 9% of the time, Pallas kernels for 15%

profile of v3, /device:TPU:32, one launch (start us, length us, event | category | flops | bytes accessed | tf_op | source)
XLA Modules:
  0.0 153.3 jit_solution(7095080602751596743)
XLA Ops:
  0.0 2.0 %shard_map.92 = s32[256,128]{1,0:T(8,128)} custom-call(s32[32,4,512]{2,1,0:T(4,128)} %bitcast.23, s32[32,512]{1,0:T(8,128)} %bitcast.24, s32[1,512]{1,0:T(1,128)} %counts_ref.1), custom_call_target="tpu_custom_call" | custom-call | tf_op jit(solution)/shard_map/pallas_call | solution.py:58
  2.0 27.1 %all_to_all.10 = s32[128,2,128]{2,1,0:T(2,128)S(1)} all-to-all(s32[128,2,128]{2,1,0:T(2,128)} %bitcast.22), channel_id=1, replica_groups=mesh['dev'=128,'rep'=2] {'dev'}, dimensions={0} | all-to-all | bytes 262144 | tf_op jit(solution)/shard_map/all_to_all | solution.py:352
  29.1 0.0 copy-start
  29.1 1.6 %copy-done = bf16[4,2048,128]{2,1,0:T(8,128)(2,1)S(1)} copy-done((bf16[4,2048,128]{2,1,0:T(8,128)(2,1)S(1)}, bf16[4,2048,128]{2,1,0:T(8,128)(2,1)}, u32[]{:S(2)}) %copy-start) | copy-done | bytes 2097176
  30.7 0.0 copy-start.6
  30.7 0.0 copy-start.5
  30.7 29.1 %shard_map.93 = bf16[128,80,128]{2,1,0:T(8,128)(2,1)} custom-call(s32[256,128]{1,0:T(8,128)S(1)} %bitcast.17, bf16[8192,128]{1,0:T(8,128)(2,1)S(1)} %bitcast.18), custom_call_target="tpu_custom_call" | custom-call | flops 20000000000 | bytes 5242880 | tf_op jit(solution)/shard_map/pallas_call | solution.py:142
  59.8 6.5 %all-to-all-start.1 = ((bf16[128,80,128]{2,1,0:T(8,128)(2,1)}), bf16[128,80,128]{2,1,0:T(8,128)(2,1)S(1)}, u32[]{:S(2)}, u32[]{:S(2)}) async-start(bf16[128,80,128]{2,1,0:T(8,128)(2,1)} %shard_map.93), calls=%async_computation.1 | async-start | bytes 5242880 | tf_op jit(solution)/shard_map/all_to_all | solution.py:357
  66.3 0.5 broadcast.37
  66.8 0.0 copy-done.6
  66.8 0.7 reduce.3
  67.5 0.1 reshape_squeeze.5
  67.6 0.2 reduce_window_sum.13
  67.8 0.1 reduce_window_sum.14
  67.9 0.1 add.32
  68.0 0.1 add.33
  68.1 0.0 copy-done.5
  68.1 0.1 copy.15
  68.2 0.0 copy-start.7
  68.3 11.3 %copy.19 = bf16[512,16,512]{2,0,1:T(8,128)(2,1)} copy(bf16[512,16,512]{2,1,0:T(8,128)(2,1)} %bitcast.20) | data formatting | bytes 16777216 | tf_op jit(solution)/shard_map/reshape | solution.py:370
  79.6 0.0 copy-done.7
  79.6 0.3 select_reduce_fusion
  79.9 0.2 convert_bitcast_fusion.pos_ref
  80.1 0.0 copy-start.1
  80.1 0.0 copy-start.2
  80.1 23.5 %shard_map.91.selector_ref = bf16[64,512,256]{2,1,0:T(8,128)(2,1)S(1)} custom-call(f32[512,128]{1,0:T(8,128)S(1)} %convert_bitcast_fusion.pos_ref), custom_call_target="tpu_custom_call" | custom-call | flops 10000000000 | bytes 16777216 | tf_op jit(solution)/shard_map/pallas_call | solution.py:195
  103.6 0.0 copy-start.3
  103.7 5.7 %copy-done.3 = bf16[64,512,256]{2,1,0:T(8,128)(2,1)} copy-done((bf16[64,512,256]{2,1,0:T(8,128)(2,1)}, bf16[64,512,256]{2,1,0:T(8,128)(2,1)S(1)}, u32[]{:S(2)}) %copy-start.3) | copy-done | bytes 16777240
  109.4 20.0 %all-to-all-done.1.refs_0_ = bf16[128,80,128]{2,1,0:T(8,128)(2,1)S(1)} async-done(((bf16[128,80,128]{2,1,0:T(8,128)(2,1)}), bf16[128,80,128]{2,1,0:T(8,128)(2,1)S(1)}, u32[]{:S(2)}, u32[]{:S(2)}) %all-to-all-start.1) | async-done | bytes 2621472 | tf_op jit(solution)/shard_map/all_to_all | solution.py:357
  129.4 0.0 copy-start.4
  129.4 1.6 %copy-done.4 = bf16[128,80,128]{2,1,0:T(8,128)(2,1)} copy-done((bf16[128,80,128]{2,1,0:T(8,128)(2,1)}, bf16[128,80,128]{2,1,0:T(8,128)(2,1)S(1)}, u32[]{:S(2)}) %copy-start.4) | copy-done | bytes 2621464
  131.0 0.0 copy-done.1
  131.0 0.0 copy-done.2
  131.0 22.1 %shard_map.94 = bf16[128,512]{1,0:T(8,128)(2,1)} custom-call(s32[512]{0:T(512)S(1)} %get-tuple-element.6.base_ref, bf16[64,512,256]{2,1,0:T(8,128)(2,1)} %copy-done.3, bf16[16,512]{1,0:T(8,128)(2,1)S(1)} %copy-done.1, bf16[16,512,512]{2,1,0:T(8,128)(2,1)} %bitcast.21, f32[1,512]{1,0:T(1,128)S(1)} %bitcast.19, bf16[128,80,128]{2,1,0:T(8,128)(2,1)} %copy-done.4), custom_call_target="tpu_custom_call" | custom-call | flops 20000000000 | bytes 16777216 | tf_op jit(solution)/shard_map/pallas_call | solution.py:322
  (3 shorter events, 0.0 us)
Async XLA Ops:
  29.1 1.6 %copy-start = (bf16[4,2048,128]{2,1,0:T(8,128)(2,1)S(1)}, bf16[4,2048,128]{2,1,0:T(8,128)(2,1)}, u32[]{:S(2)}) copy-start(bf16[4,2048,128]{2,1,0:T(8,128)(2,1)} %param.9) | copy-start | bytes 6291460
  30.7 36.1 %copy-start.6 = (s32[1,512]{1,0:T(1,128)S(1)}, s32[1,512]{1,0:T(1,128)}, u32[]{:S(2)}) copy-start(s32[1,512]{1,0:T(1,128)} %counts_ref.1) | copy-start | bytes 6148
  30.7 37.4 %copy-start.5 = (s32[128,512]{1,0:T(8,128)S(1)}, s32[128,512]{1,0:T(8,128)}, u32[]{:S(2)}) copy-start(s32[128,512]{1,0:T(8,128)} %param.13) | copy-start | bytes 786436
  59.8 69.6 %all-to-all-start.1 = ((bf16[128,80,128]{2,1,0:T(8,128)(2,1)}), bf16[128,80,128]{2,1,0:T(8,128)(2,1)S(1)}, u32[]{:S(2)}, u32[]{:S(2)}) async-start(bf16[128,80,128]{2,1,0:T(8,128)(2,1)} %shard_map.93), calls=%async_computation.1 | async-start | bytes 5242880 | tf_op jit(solution)/shard_map/all_to_all | solution.py:357
  68.2 11.4 %copy-start.7 = (s32[512]{0:T(512)S(1)}, s32[512]{0:T(512)}, u32[]{:S(2)}) copy-start(s32[512]{0:T(512)} %param.14) | copy-start | bytes 6148
  80.1 50.8 %copy-start.1 = (bf16[16,512]{1,0:T(8,128)(2,1)S(1)}, bf16[16,512]{1,0:T(8,128)(2,1)}, u32[]{:S(2)}) copy-start(bf16[16,512]{1,0:T(8,128)(2,1)} %compress_ref.1) | copy-start | bytes 49156
  80.1 50.8 %copy-start.2 = (f32[512]{0:T(512)S(1)}, f32[512]{0:T(512)}, u32[]{:S(2)}) copy-start(f32[512]{0:T(512)} %param.17) | copy-start | bytes 6148
  103.6 5.7 %copy-start.3 = (bf16[64,512,256]{2,1,0:T(8,128)(2,1)}, bf16[64,512,256]{2,1,0:T(8,128)(2,1)S(1)}, u32[]{:S(2)}) copy-start(bf16[64,512,256]{2,1,0:T(8,128)(2,1)S(1)} %shard_map.91.selector_ref) | copy-start | bytes 50331652
  129.4 1.6 %copy-start.4 = (bf16[128,80,128]{2,1,0:T(8,128)(2,1)}, bf16[128,80,128]{2,1,0:T(8,128)(2,1)S(1)}, u32[]{:S(2)}) copy-start(bf16[128,80,128]{2,1,0:T(8,128)(2,1)S(1)} %all-to-all-done.1.refs_0_) | copy-start | bytes 7864324

commit v4 on v3

--- a/solution.py
+++ b/solution.py
@@ -10,7 +10,8 @@
 PACK_ROOM = 80
 CHUNKS = ((0, 80),)
 BLOCK = 8
-PARTS = 4
+PARTS = 8
+SENDERS = 2
 GROUP = 4
 
 
@@ -109,21 +110,25 @@
 
     lax.fori_loop(0, vocab_rows // 256, widen, 0)
 
-    def one_sender(d, carry):
-        views = [ids_smem.at[pl.ds(d * lines + q, 1)] for q in range(lines)]
+    def some_senders(i, carry):
+        views = [
+            [ids_smem.at[pl.ds((i * SENDERS + n) * lines + q, 1)] for q in range(lines)]
+            for n in range(SENDERS)
+        ]
         for j in range(rows):
-            parts = [
-                table_f32[pl.ds(views[p // per][0, (p % per) * rows + j], 1), :]
-                for p in range(pool)
-            ]
-            while len(parts) > 1:
-                parts = [parts[i] + parts[i + 1] for i in range(0, len(parts), 2)]
-            pooled[pl.ds(d * rows + j, 1), :] = parts[0]
+            for n in range(SENDERS):
+                parts = [
+                    table_f32[pl.ds(views[n][p // per][0, (p % per) * rows + j], 1), :]
+                    for p in range(pool)
+                ]
+                while len(parts) > 1:
+                    parts = [parts[m] + parts[m + 1] for m in range(0, len(parts), 2)]
+                pooled[pl.ds((i * SENDERS + n) * rows + j, 1), :] = parts[0]
         return carry
 
     for c in range(shares):
         copies[c].wait()
-        lax.fori_loop(c * step, (c + 1) * step, one_sender, 0)
+        lax.fori_loop(c * step // SENDERS, (c + 1) * step // SENDERS, some_senders, 0)
 
     def narrow(d, carry):
         at = pl.multiple_of(d * rows, 8)
@@ -153,7 +158,7 @@
             pltpu.SemaphoreType.DMA((4,)),
             pltpu.SemaphoreType.DMA(()),
         ],
-        compiler_params=pltpu.CompilerParams(vmem_limit_bytes=24 << 20),
+        compiler_params=pltpu.CompilerParams(vmem_limit_bytes=125 << 19),
         cost_estimate=pl.CostEstimate(flops=20_000_000_000, bytes_accessed=5 << 20, transcendentals=0),
     )(message.reshape(peers * halves, width), table_rows)
 
@@ -335,7 +340,7 @@
             pltpu.SemaphoreType.DMA((PARTS,)),
             pltpu.SemaphoreType.DMA(()),
         ],
-        compiler_params=pltpu.CompilerParams(vmem_limit_bytes=53 << 20),
+        compiler_params=pltpu.CompilerParams(vmem_limit_bytes=125 << 19),
         cost_estimate=pl.CostEstimate(flops=20_000_000_000, bytes_accessed=16 << 20, transcendentals=0),
     )(base, selectors, compress, weight, bias, *arrived)
 

time: 154 us -> 151 us (0.981)
  local copies, waits for them, and re-layouts: 21.3 us -> 18.1 us
    unnamed x18 -> x10, local copies, waits for them, and re-layouts: 9.53 us -> 6.35 us
  transfers between devices with their start and end apart: 1 -> 1, of which waited for: 1 -> 1; matrix products, arithmetic and copies ran while one was open for 9% -> 10% of each run, Pallas kernels for 15% -> 16%
where the time goes in v4:
time: 151 us; the launch traced here: 150 us
  Pallas kernels  75.9 us (50%)
  blocking collectives  27.1 us (18%)
  waiting for transfers between devices  19.2 us (13%)
  local copies, waits for them, and re-layouts  18.1 us (12%)
  starting transfers between devices  7.61 us (5%)
  other arithmetic  1.91 us (1%)
    pallas_call x1, Pallas kernels, pool_rows(): pl.pallas_call(functools.partial(pool_kernel, first=first, rows=rows, poo...  28.6 us
    all_to_all x1, blocking collectives, shards(): lax.all_to_all(message, 'dev', split_axis=0, concat_axis=0, tiled=True)  27.1 us
    pallas_call x1, Pallas kernels, build_selectors(): pl.pallas_call(selector_kernel, grid=(blocks // some,), out_shape=jax.Sha...  23.5 us
    pallas_call x1, Pallas kernels, score_samples(): pl.pallas_call(functools.partial(tail_kernel, most_rows=most_rows), out_s...  21.8 us
    all_to_all x1, waiting for transfers between devices, shards(): lax.all_to_all(pooled, 'dev', split_axis=0, concat_axis=0, tiled=True)  19.2 us
    reshape x1, local copies, waits for them, and re-layouts, shards(): weight = jnp.transpose(top_weight.reshape(slots, mixes, -1), (1, 0, 2))  11.3 us
    all_to_all x1, starting transfers between devices, shards(): lax.all_to_all(pooled, 'dev', split_axis=0, concat_axis=0, tiled=True)  7.61 us
    unnamed x10, local copies, waits for them, and re-layouts  6.35 us
  transfers between devices with their start and end apart: 1, of which 1 were waited for; matrix products, arithmetic and copies ran while one was open for 10% of the time, Pallas kernels for 16%

profile of v4, /device:TPU:32, one launch (start us, length us, event | category | flops | bytes accessed | tf_op | source)
XLA Modules:
  0.0 150.2 jit_solution(16932372256276761398)
XLA Ops:
  0.0 2.0 %shard_map.92 = s32[256,128]{1,0:T(8,128)} custom-call(s32[32,4,512]{2,1,0:T(4,128)} %bitcast.20, s32[32,512]{1,0:T(8,128)} %bitcast.22, s32[1,512]{1,0:T(1,128)} %counts_ref.1), custom_call_target="tpu_custom_call" | custom-call | tf_op jit(solution)/shard_map/pallas_call | solution.py:59
  2.0 27.1 %all_to_all.10 = s32[128,2,128]{2,1,0:T(2,128)} all-to-all(s32[128,2,128]{2,1,0:T(2,128)} %bitcast.19), channel_id=1, replica_groups=mesh['dev'=128,'rep'=2] {'dev'}, dimensions={0} | all-to-all | bytes 262144 | tf_op jit(solution)/shard_map/all_to_all | solution.py:357
  29.1 0.0 copy-start.2
  29.1 0.0 copy-start.1
  29.1 28.6 %shard_map.93 = bf16[128,80,128]{2,1,0:T(8,128)(2,1)} custom-call(s32[256,128]{1,0:T(8,128)} %bitcast.21, bf16[8192,128]{1,0:T(8,128)(2,1)} %bitcast.25), custom_call_target="tpu_custom_call" | custom-call | flops 20000000000 | bytes 5242880 | tf_op jit(solution)/shard_map/pallas_call | solution.py:147
  57.8 7.6 %all-to-all-start.1 = ((bf16[128,80,128]{2,1,0:T(8,128)(2,1)}), bf16[128,80,128]{2,1,0:T(8,128)(2,1)}, u32[]{:S(2)}, u32[]{:S(2)}) async-start(bf16[128,80,128]{2,1,0:T(8,128)(2,1)} %shard_map.93), calls=%async_computation.1 | async-start | bytes 5242880 | tf_op jit(solution)/shard_map/all_to_all | solution.py:362
  65.4 0.5 broadcast.37
  65.9 0.0 copy-done.2
  65.9 0.7 reduce.3
  66.6 0.1 reshape_squeeze.5
  66.7 0.2 reduce_window_sum.13
  66.9 0.1 reduce_window_sum.14
  67.0 0.1 add.32
  67.1 0.1 add.33
  67.2 0.0 copy-done.1
  67.2 0.1 copy.15
  67.3 0.0 copy-start.3
  67.3 11.3 %copy.19 = bf16[512,16,512]{2,0,1:T(8,128)(2,1)} copy(bf16[512,16,512]{2,1,0:T(8,128)(2,1)} %bitcast.17) | data formatting | bytes 16777216 | tf_op jit(solution)/shard_map/reshape | solution.py:375
  78.7 0.0 copy-done.3
  78.7 0.9 select_reduce_fusion
  79.6 0.2 convert_bitcast_fusion.pos_ref
  79.8 23.5 %shard_map.91.selector_ref = bf16[64,512,256]{2,1,0:T(8,128)(2,1)S(1)} custom-call(f32[512,128]{1,0:T(8,128)S(1)} %convert_bitcast_fusion.pos_ref), custom_call_target="tpu_custom_call" | custom-call | flops 10000000000 | bytes 16777216 | tf_op jit(solution)/shard_map/pallas_call | solution.py:200
  103.3 0.0 copy-start
  103.3 5.7 %copy-done = bf16[64,512,256]{2,1,0:T(8,128)(2,1)} copy-done((bf16[64,512,256]{2,1,0:T(8,128)(2,1)}, bf16[64,512,256]{2,1,0:T(8,128)(2,1)S(1)}, u32[]{:S(2)}) %copy-start) | copy-done | bytes 16777240
  109.0 19.2 %all-to-all-done.1.refs_0_ = bf16[128,80,128]{2,1,0:T(8,128)(2,1)} async-done(((bf16[128,80,128]{2,1,0:T(8,128)(2,1)}), bf16[128,80,128]{2,1,0:T(8,128)(2,1)}, u32[]{:S(2)}, u32[]{:S(2)}) %all-to-all-start.1) | async-done | bytes 2621472 | tf_op jit(solution)/shard_map/all_to_all | solution.py:362
  128.2 21.8 %shard_map.94 = bf16[128,512]{1,0:T(8,128)(2,1)} custom-call(s32[512]{0:T(512)} %get-tuple-element.6.base_ref, bf16[64,512,256]{2,1,0:T(8,128)(2,1)} %copy-done, bf16[16,512]{1,0:T(8,128)(2,1)} %compress_ref.1, bf16[16,512,512]{2,1,0:T(8,128)(2,1)} %bitcast.18, f32[1,512]{1,0:T(1,128)} %bitcast.26, bf16[128,80,128]{2,1,0:T(8,128)(2,1)} %all-to-all-done.1.refs_0_), custom_call_target="tpu_custom_call" | custom-call | flops 20000000000 | bytes 16777216 | tf_op jit(solution)/shard_map/pallas_call | solution.py:327
  (3 shorter events, 0.0 us)
Async XLA Ops:
  29.1 36.8 %copy-start.2 = (s32[1,512]{1,0:T(1,128)S(1)}, s32[1,512]{1,0:T(1,128)}, u32[]{:S(2)}) copy-start(s32[1,512]{1,0:T(1,128)} %counts_ref.1) | copy-start | bytes 6148
  29.1 38.1 %copy-start.1 = (s32[128,512]{1,0:T(8,128)S(1)}, s32[128,512]{1,0:T(8,128)}, u32[]{:S(2)}) copy-start(s32[128,512]{1,0:T(8,128)} %param.13) | copy-start | bytes 786436
  57.8 70.5 %all-to-all-start.1 = ((bf16[128,80,128]{2,1,0:T(8,128)(2,1)}), bf16[128,80,128]{2,1,0:T(8,128)(2,1)}, u32[]{:S(2)}, u32[]{:S(2)}) async-start(bf16[128,80,128]{2,1,0:T(8,128)(2,1)} %shard_map.93), calls=%async_computation.1 | async-start | bytes 5242880 | tf_op jit(solution)/shard_map/all_to_all | solution.py:362
  67.3 11.4 %copy-start.3 = (s32[512]{0:T(512)S(1)}, s32[512]{0:T(512)}, u32[]{:S(2)}) copy-start(s32[512]{0:T(512)} %param.14) | copy-start | bytes 6148
  103.3 5.7 %copy-start = (bf16[64,512,256]{2,1,0:T(8,128)(2,1)}, bf16[64,512,256]{2,1,0:T(8,128)(2,1)S(1)}, u32[]{:S(2)}) copy-start(bf16[64,512,256]{2,1,0:T(8,128)(2,1)S(1)} %shard_map.91.selector_ref) | copy-start | bytes 50331652

commit v5 on v4

--- a/solution.py
+++ b/solution.py
@@ -8,10 +8,12 @@
 from jax.sharding import PartitionSpec as P
 
 PACK_ROOM = 80
-CHUNKS = ((0, 80),)
 BLOCK = 8
 PARTS = 8
+AHEAD = 3
+WEIGHTS_AT = 5
 SENDERS = 2
+SHARES = 8
 GROUP = 4
 
 
@@ -67,7 +69,8 @@
 
 
 def pool_kernel(
-    msg_ref, table_hbm, out_ref, table_ref, table_f32, pooled, ids, ids_smem, sems, table_sem,
+    msg_ref, table_hbm, out_hbm, table_ref, table_f32, pooled, out_ref, ids, ids_smem, sems,
+    out_sems, table_sem,
     *, first, rows, pool,
 ):
     vocab_rows, emb = table_hbm.shape
@@ -126,16 +129,24 @@
                 pooled[pl.ds((i * SENDERS + n) * rows + j, 1), :] = parts[0]
         return carry
 
+    def narrow(d, carry):
+        at = pl.multiple_of(d * rows, 8)
+        out_ref[d] = pooled[pl.ds(at, rows), :].astype(jnp.bfloat16)
+        return carry
+
+    outs = [
+        pltpu.make_async_copy(
+            out_ref.at[pl.ds(c * step, step)], out_hbm.at[pl.ds(c * step, step)], out_sems.at[c]
+        )
+        for c in range(shares)
+    ]
     for c in range(shares):
         copies[c].wait()
         lax.fori_loop(c * step // SENDERS, (c + 1) * step // SENDERS, some_senders, 0)
-
-    def narrow(d, carry):
-        at = pl.multiple_of(d * rows, 8)
-        out_ref[d] = pooled[pl.ds(at, rows), :].astype(jnp.bfloat16)
-        return carry
-
-    lax.fori_loop(0, peers, narrow, 0, unroll=4)
+        lax.fori_loop(c * step, (c + 1) * step, narrow, 0, unroll=4)
+        outs[c].start()
+    for c in range(shares):
+        outs[c].wait()
 
 
 def pool_rows(message, table_rows, first, rows):
@@ -148,14 +159,16 @@
         functools.partial(pool_kernel, first=first, rows=rows, pool=pool),
         out_shape=jax.ShapeDtypeStruct((peers, rows, emb), jnp.bfloat16),
         in_specs=[vmem, pl.BlockSpec(memory_space=pltpu.HBM)],
-        out_specs=vmem,
+        out_specs=pl.BlockSpec(memory_space=pltpu.HBM),
         scratch_shapes=[
             pltpu.VMEM(table_rows.shape, jnp.bfloat16),
             pltpu.VMEM((table_rows.shape[0] + 8, emb), jnp.float32),
             pltpu.VMEM((peers * rows, emb), jnp.float32),
+            pltpu.VMEM((peers, rows, emb), jnp.bfloat16),
             pltpu.VMEM((peers * lines, width), jnp.int32),
             pltpu.SMEM((peers * lines, width), jnp.int32),
-            pltpu.SemaphoreType.DMA((4,)),
+            pltpu.SemaphoreType.DMA((SHARES,)),
+            pltpu.SemaphoreType.DMA((SHARES,)),
             pltpu.SemaphoreType.DMA(()),
         ],
         compiler_params=pltpu.CompilerParams(vmem_limit_bytes=125 << 19),
@@ -166,7 +179,7 @@
 def selector_kernel(pos_ref, out_ref):
     blocks, rows, lanes = out_ref.shape
     pairs = rows // BLOCK
-    half = lanes // 2
+    half = lanes
     lane = lax.broadcasted_iota(jnp.int32, (BLOCK, half), 1).astype(jnp.float32)
     upper = lax.broadcasted_iota(jnp.int32, (BLOCK, pos_ref.shape[1]), 0) < BLOCK // 2
 
@@ -178,15 +191,17 @@
             jnp.where(upper, here, pltpu.roll(swapped, samples - 1, 1)),
             jnp.where(upper, swapped, pltpu.roll(here, samples - 1, 1)),
         )
-        for side, pos in enumerate(sides):
-            for p in range(0, pairs, 2):
-                both = [
-                    jnp.where(jnp.broadcast_to(pos[:, c : c + 1], (BLOCK, half)) == lane, 1.0, 0.0)
-                    for c in (2 * p, 2 * p + 2)
+        for p in range(0, pairs, 2):
+            both = []
+            for c in (2 * p, 2 * p + 2):
+                marks = [
+                    jnp.where(jnp.broadcast_to(pos[:, c : c + 1], (BLOCK, half)) == lane, mark, 0.0)
+                    for mark, pos in zip((1.0, 2.0), sides)
                 ]
-                out_ref[i, pl.ds(p * BLOCK, 2 * BLOCK), pl.ds(side * half, half)] = (
-                    jnp.concatenate(both, axis=0).astype(jnp.bfloat16)
-                )
+                both.append(marks[0] + marks[1])
+            out_ref[i, pl.ds(p * BLOCK, 2 * BLOCK), :] = jnp.concatenate(both, axis=0).astype(
+                jnp.bfloat16
+            )
         return carry
 
     lax.fori_loop(0, blocks, one_block, 0)
@@ -200,26 +215,35 @@
     return pl.pallas_call(
         selector_kernel,
         grid=(blocks // some,),
-        out_shape=jax.ShapeDtypeStruct((blocks, pairs * BLOCK, 256), jnp.bfloat16),
+        out_shape=jax.ShapeDtypeStruct((blocks, pairs * BLOCK, 128), jnp.bfloat16),
         in_specs=[pl.BlockSpec((some * BLOCK, samples), lambda i: (i, 0))],
-        out_specs=pl.BlockSpec((some, pairs * BLOCK, 256), lambda i: (i, 0, 0)),
+        out_specs=pl.BlockSpec((some, pairs * BLOCK, 128), lambda i: (i, 0, 0)),
         compiler_params=pltpu.CompilerParams(vmem_limit_bytes=8 << 20),
-        cost_estimate=pl.CostEstimate(flops=10_000_000_000, bytes_accessed=16 << 20, transcendentals=0),
+        cost_estimate=pl.CostEstimate(flops=10_000_000_000, bytes_accessed=8 << 20, transcendentals=0),
     )(pos)
 
 
-def tail_kernel(base_ref, selector_ref, compress_ref, weight_ref, bias_ref, *refs, most_rows):
-    row_refs = refs[: len(CHUNKS)]
-    (
-        out_ref, rows_f32, feats, pairs, turned, select_vmem, weight_vmem, select_sem, weight_sem,
-    ) = refs[len(CHUNKS) :]
-    groups, _, emb = row_refs[0].shape
+def tail_kernel(
+    base_ref, selector_ref, compress_ref, weight_ref, bias_ref, arrived_ref, out_ref,
+    rows_bf16, rows_f32, feats, pairs, turned, select_vmem, weight_vmem,
+    row_sem, select_sem, weight_sem, *, most_rows,
+):
+    groups, _, emb = arrived_ref.shape
     total_rows = groups * PACK_ROOM
     sample_pairs, _, features, _ = feats.shape
     samples = 2 * sample_pairs
     mixes = compress_ref.shape[0]
     blocks = features // BLOCK
     share = blocks // PARTS
+    quarter = groups // 4
+    row_copies = [
+        pltpu.make_async_copy(
+            arrived_ref.at[pl.ds(c * quarter, quarter)],
+            rows_bf16.at[pl.ds(c * quarter, quarter)],
+            row_sem.at[c],
+        )
+        for c in range(4)
+    ]
     copies = [
         pltpu.make_async_copy(
             selector_ref.at[pl.ds(part * share, share)],
@@ -228,24 +252,29 @@
         )
         for part in range(PARTS)
     ]
-    for copy in copies:
+    weight_copy = pltpu.make_async_copy(weight_ref, weight_vmem, weight_sem)
+    for copy in row_copies + copies[:1]:
         copy.start()
-    weight_copy = pltpu.make_async_copy(weight_ref, weight_vmem, weight_sem)
-    weight_copy.start()
 
     rows_f32[pl.ds(total_rows, most_rows), :] = jnp.zeros((most_rows, emb), jnp.float32)
 
     def widen(g, carry):
-        for (first, count), row_ref in zip(CHUNKS, row_refs):
-            at = pl.multiple_of(g * PACK_ROOM + first, 16)
-            rows_f32[pl.ds(at, count), :] = row_ref[g].astype(jnp.float32)
-        return carry
-
-    lax.fori_loop(0, groups, widen, 0, unroll=4)
+        at = pl.multiple_of(g * PACK_ROOM, 16)
+        rows_f32[pl.ds(at, PACK_ROOM), :] = rows_bf16[g].astype(jnp.float32)
+        return carry
+
+    for c in range(4):
+        row_copies[c].wait()
+        lax.fori_loop(c * quarter, (c + 1) * quarter, widen, 0, unroll=4)
+    for copy in copies[1:AHEAD]:
+        copy.start()
 
     first_half = lax.broadcasted_iota(jnp.int32, (1, BLOCK, emb), 1) < BLOCK // 2
     some = 32
     empty = jnp.zeros((BLOCK // 2 * most_rows, emb), jnp.bfloat16)
+    zero = jnp.zeros((some * BLOCK, BLOCK // 2 * most_rows), jnp.bfloat16)
+    one = jnp.ones_like(zero)
+    two = one + one
 
     def expand(i, carry):
         for pair in range(2):
@@ -266,7 +295,9 @@
             for c in range(sample_pairs // some):
                 even, odd = [], []
                 for block, rhs in tops:
-                    lhs = select_vmem[block, pl.ds(c * some * BLOCK, some * BLOCK), :]
+                    marks = select_vmem[block, pl.ds(c * some * BLOCK, some * BLOCK), :]
+                    second = jnp.where(marks >= two, one, zero)
+                    lhs = jnp.concatenate([marks - second - second, second], axis=1)
                     got = jnp.dot(lhs, rhs, preferred_element_type=jnp.float32)
                     got = got.reshape(some, BLOCK, 2 * emb)
                     left, right = got[:, :, :emb], got[:, :, emb:]
@@ -280,6 +311,10 @@
 
     for part in range(PARTS):
         copies[part].wait()
+        if part + AHEAD < PARTS:
+            copies[part + AHEAD].start()
+        if part == WEIGHTS_AT:
+            weight_copy.start()
         lax.fori_loop(part * share // 4, (part + 1) * share // 4, expand, 0)
 
     per = 8
@@ -300,9 +335,13 @@
             second = jnp.concatenate([none, mixed[j][:, emb:]], axis=1)
             lhs = jnp.concatenate([first, second], axis=0)
             got = jnp.dot(lhs, turned[j], preferred_element_type=jnp.float32)
-            at = pl.multiple_of((i * per + 2 * j) * mixes, 2 * mixes)
-            for c in range(features // 128):
-                pairs[c, pl.ds(at, 2 * mixes), :] = got[:, c * 128 : (c + 1) * 128]
+            for n in range(2 * mixes // BLOCK):
+                sample = i * per + 2 * j + n * BLOCK // mixes
+                at = pl.multiple_of(sample * BLOCK, BLOCK)
+                for c in range(features // 128):
+                    pairs[c, n % (mixes // BLOCK), pl.ds(at, BLOCK), :] = got[
+                        n * BLOCK : (n + 1) * BLOCK, c * 128 : (c + 1) * 128
+                    ]
         return carry
 
     lax.fori_loop(0, samples // per, score, 0)
@@ -311,7 +350,11 @@
     total = jnp.broadcast_to(bias_ref[...], (samples, out_ref.shape[1]))
     for k in range(mixes):
         lhs = jnp.concatenate(
-            [pairs[c, pl.ds(k, samples, stride=mixes), :] for c in range(features // 128)], axis=1
+            [
+                pairs[c, k // BLOCK, pl.ds(k % BLOCK, samples, stride=BLOCK), :]
+                for c in range(features // 128)
+            ],
+            axis=1,
         ).astype(jnp.bfloat16)
         total = total + jnp.dot(lhs, weight_vmem[k], preferred_element_type=jnp.float32)
     out_ref[...] = jnp.maximum(total, 0.0).astype(jnp.bfloat16)
@@ -320,29 +363,30 @@
 def score_samples(base, selectors, arrived, compress, weight, bias, most_rows):
     mixes, features = compress.shape
     units = weight.shape[2]
-    groups, _, emb = arrived[0].shape
+    groups, _, emb = arrived.shape
     samples = 2 * selectors.shape[1] // BLOCK
     vmem = pl.BlockSpec(memory_space=pltpu.VMEM)
     hbm = pl.BlockSpec(memory_space=pltpu.HBM)
     return pl.pallas_call(
         functools.partial(tail_kernel, most_rows=most_rows),
         out_shape=jax.ShapeDtypeStruct((samples, units), jnp.bfloat16),
-        in_specs=[pl.BlockSpec(memory_space=pltpu.SMEM), hbm, vmem, hbm, vmem]
-        + [vmem] * len(arrived),
+        in_specs=[pl.BlockSpec(memory_space=pltpu.SMEM), hbm, vmem, hbm, vmem, hbm],
         out_specs=vmem,
         scratch_shapes=[
+            pltpu.VMEM(arrived.shape, jnp.bfloat16),
             pltpu.VMEM((groups * PACK_ROOM + most_rows, emb), jnp.float32),
             pltpu.VMEM((samples // 2, 2, features, emb), jnp.bfloat16),
-            pltpu.VMEM((features // 128, samples * mixes, 128), jnp.float32),
+            pltpu.VMEM((features // 128, mixes // BLOCK, samples * BLOCK, 128), jnp.float32),
             pltpu.VMEM((4, 2 * emb, features), jnp.bfloat16),
             pltpu.VMEM(selectors.shape, jnp.bfloat16),
             pltpu.VMEM(weight.shape, jnp.bfloat16),
+            pltpu.SemaphoreType.DMA((4,)),
             pltpu.SemaphoreType.DMA((PARTS,)),
             pltpu.SemaphoreType.DMA(()),
         ],
         compiler_params=pltpu.CompilerParams(vmem_limit_bytes=125 << 19),
         cost_estimate=pl.CostEstimate(flops=20_000_000_000, bytes_accessed=16 << 20, transcendentals=0),
-    )(base, selectors, compress, weight, bias, *arrived)
+    )(base, selectors, compress, weight, bias, arrived)
 
 
 def shards(
@@ -356,10 +400,8 @@
     message = bag_message(bag_rows[0], bag_lengths[0], row_counts, vocabulary)
     got = lax.all_to_all(message, "dev", split_axis=0, concat_axis=0, tiled=True)
     table_rows = tables.reshape(-1, emb)
-    arrived = []
-    for first, count in CHUNKS:
-        pooled = pool_rows(got, table_rows, first, count)
-        arrived.append(lax.all_to_all(pooled, "dev", split_axis=0, concat_axis=0, tiled=True))
+    pooled = pool_rows(got, table_rows, 0, PACK_ROOM)
+    arrived = lax.all_to_all(pooled, "dev", split_axis=0, concat_axis=0, tiled=True)
 
     grouped = counts.reshape(-1, GROUP)
     before = jnp.cumsum(grouped, axis=1) - grouped

time: 151 us -> 148 us (0.980)
  waiting for transfers between devices: 19.2 us -> 22.2 us
  Pallas kernels: 75.9 us -> 73.2 us
  local copies, waits for them, and re-layouts: 18.1 us -> 15.6 us
    all_to_all x1, waiting for transfers between devices: 19.2 us -> 22.2 us  [shards(): lax.all_to_all(pooled, 'dev', split_axis=0, concat_axis=0, tiled=True)]
    unnamed x10, local copies, waits for them, and re-layouts: 6.35 us -> 3.86 us
    pallas_call x1, Pallas kernels: 21.8 us -> 20.2 us  [score_samples(): pl.pallas_call(functools.partial(tail_kernel, most_rows=most_rows), out_s...]
where the time goes in v5:
time: 148 us
  Pallas kernels  73.2 us (49%)
  blocking collectives  27.1 us (18%)
  waiting for transfers between devices  22.2 us (15%)
  local copies, waits for them, and re-layouts  15.6 us (11%)
  starting transfers between devices  7.61 us (5%)
  other arithmetic  1.91 us (1%)
    pallas_call x1, Pallas kernels, pool_rows(): pl.pallas_call(functools.partial(pool_kernel, first=first, rows=rows, poo...  27.9 us
    all_to_all x1, blocking collectives, shards(): lax.all_to_all(message, 'dev', split_axis=0, concat_axis=0, tiled=True)  27.1 us
    pallas_call x1, Pallas kernels, build_selectors(): pl.pallas_call(selector_kernel, grid=(blocks // some,), out_shape=jax.Sha...  23 us
    all_to_all x1, waiting for transfers between devices, shards(): lax.all_to_all(pooled, 'dev', split_axis=0, concat_axis=0, tiled=True)  22.2 us
    pallas_call x1, Pallas kernels, score_samples(): pl.pallas_call(functools.partial(tail_kernel, most_rows=most_rows), out_s...  20.2 us
    reshape x1, local copies, waits for them, and re-layouts, shards(): weight = jnp.transpose(top_weight.reshape(slots, mixes, -1), (1, 0, 2))  11.3 us
    all_to_all x1, starting transfers between devices, shards(): lax.all_to_all(pooled, 'dev', split_axis=0, concat_axis=0, tiled=True)  7.61 us
    unnamed x10, local copies, waits for them, and re-layouts  3.86 us
  transfers between devices with their start and end apart: 1, of which 1 were waited for; matrix products, arithmetic and copies ran while one was open for 10% of the time, Pallas kernels for 16%

profile of v5, /device:TPU:32, one launch (start us, length us, event | category | flops | bytes accessed | tf_op | source)
XLA Modules:
  0.0 147.9 jit_solution(9716673775967694315)
XLA Ops:
  0.0 2.0 %shard_map.92 = s32[256,128]{1,0:T(8,128)} custom-call(s32[32,4,512]{2,1,0:T(4,128)} %bitcast.20, s32[32,512]{1,0:T(8,128)} %bitcast.22, s32[1,512]{1,0:T(1,128)} %counts_ref.1), custom_call_target="tpu_custom_call" | custom-call | tf_op jit(solution)/shard_map/pallas_call | solution.py:61
  2.0 27.1 %all_to_all.10 = s32[128,2,128]{2,1,0:T(2,128)} all-to-all(s32[128,2,128]{2,1,0:T(2,128)} %bitcast.19), channel_id=1, replica_groups=mesh['dev'=128,'rep'=2] {'dev'}, dimensions={0} | all-to-all | bytes 262144 | tf_op jit(solution)/shard_map/all_to_all | solution.py:401
  29.1 0.0 copy-start.2
  29.1 0.0 copy-start.1
  29.1 27.9 %shard_map.93 = bf16[128,80,128]{2,1,0:T(8,128)(2,1)} custom-call(s32[256,128]{1,0:T(8,128)} %bitcast.21, bf16[8192,128]{1,0:T(8,128)(2,1)} %bitcast.25), custom_call_target="tpu_custom_call" | custom-call | flops 20000000000 | bytes 5242880 | tf_op jit(solution)/shard_map/pallas_call | solution.py:158
  57.1 7.6 %all-to-all-start.1 = ((bf16[128,80,128]{2,1,0:T(8,128)(2,1)}), bf16[128,80,128]{2,1,0:T(8,128)(2,1)}, u32[]{:S(2)}, u32[]{:S(2)}) async-start(bf16[128,80,128]{2,1,0:T(8,128)(2,1)} %shard_map.93), calls=%async_computation.1 | async-start | bytes 5242880 | tf_op jit(solution)/shard_map/all_to_all | solution.py:404
  64.7 0.5 broadcast.37
  65.2 0.0 copy-done.2
  65.2 0.7 reduce.3
  65.9 0.1 reshape_squeeze.5
  66.0 0.2 reduce_window_sum.13
  66.2 0.1 reduce_window_sum.14
  66.3 0.1 add.32
  66.4 0.1 add.33
  66.5 0.0 copy-done.1
  66.5 0.1 copy.15
  66.6 0.0 copy-start.3
  66.6 11.3 %copy.19 = bf16[512,16,512]{2,0,1:T(8,128)(2,1)} copy(bf16[512,16,512]{2,1,0:T(8,128)(2,1)} %bitcast.17) | data formatting | bytes 16777216 | tf_op jit(solution)/shard_map/reshape | solution.py:417
  78.0 0.0 copy-done.3
  78.0 0.9 select_reduce_fusion
  78.9 0.2 convert_bitcast_fusion.pos_ref
  79.1 23.0 %shard_map.91.selector_ref = bf16[64,512,128]{2,1,0:T(8,128)(2,1)S(1)} custom-call(f32[512,128]{1,0:T(8,128)S(1)} %convert_bitcast_fusion.pos_ref), custom_call_target="tpu_custom_call" | custom-call | flops 10000000000 | bytes 8388608 | tf_op jit(solution)/shard_map/pallas_call | solution.py:215
  102.1 0.0 copy-start
  102.1 3.2 %copy-done = bf16[64,512,128]{2,1,0:T(8,128)(2,1)} copy-done((bf16[64,512,128]{2,1,0:T(8,128)(2,1)}, bf16[64,512,128]{2,1,0:T(8,128)(2,1)S(1)}, u32[]{:S(2)}) %copy-start) | copy-done | bytes 8388632
  105.3 22.2 %all-to-all-done.1.arrived_ref = bf16[128,80,128]{2,1,0:T(8,128)(2,1)} async-done(((bf16[128,80,128]{2,1,0:T(8,128)(2,1)}), bf16[128,80,128]{2,1,0:T(8,128)(2,1)}, u32[]{:S(2)}, u32[]{:S(2)}) %all-to-all-start.1) | async-done | bytes 2621472 | tf_op jit(solution)/shard_map/all_to_all | solution.py:404
  127.5 20.2 %shard_map.94 = bf16[128,512]{1,0:T(8,128)(2,1)} custom-call(s32[512]{0:T(512)} %get-tuple-element.6.base_ref, bf16[64,512,128]{2,1,0:T(8,128)(2,1)} %copy-done, bf16[16,512]{1,0:T(8,128)(2,1)} %compress_ref.1, bf16[16,512,512]{2,1,0:T(8,128)(2,1)} %bitcast.18, f32[1,512]{1,0:T(1,128)} %bitcast.26, bf16[128,80,128]{2,1,0:T(8,128)(2,1)} %all-to-all-done.1.arrived_ref), custom_call_target="tpu_custom_call" | custom-call | flops 20000000000 | bytes 16777216 | tf_op jit(solution)/shard_map/pallas_call | solution.py:370
  (3 shorter events, 0.0 us)
Async XLA Ops:
  29.1 36.1 %copy-start.2 = (s32[1,512]{1,0:T(1,128)S(1)}, s32[1,512]{1,0:T(1,128)}, u32[]{:S(2)}) copy-start(s32[1,512]{1,0:T(1,128)} %counts_ref.1) | copy-start | bytes 6148
  29.1 37.4 %copy-start.1 = (s32[128,512]{1,0:T(8,128)S(1)}, s32[128,512]{1,0:T(8,128)}, u32[]{:S(2)}) copy-start(s32[128,512]{1,0:T(8,128)} %param.13) | copy-start | bytes 786436
  57.1 70.4 %all-to-all-start.1 = ((bf16[128,80,128]{2,1,0:T(8,128)(2,1)}), bf16[128,80,128]{2,1,0:T(8,128)(2,1)}, u32[]{:S(2)}, u32[]{:S(2)}) async-start(bf16[128,80,128]{2,1,0:T(8,128)(2,1)} %shard_map.93), calls=%async_computation.1 | async-start | bytes 5242880 | tf_op jit(solution)/shard_map/all_to_all | solution.py:404
  66.6 11.4 %copy-start.3 = (s32[512]{0:T(512)S(1)}, s32[512]{0:T(512)}, u32[]{:S(2)}) copy-start(s32[512]{0:T(512)} %param.14) | copy-start | bytes 6148
  102.1 3.2 %copy-start = (bf16[64,512,128]{2,1,0:T(8,128)(2,1)}, bf16[64,512,128]{2,1,0:T(8,128)(2,1)S(1)}, u32[]{:S(2)}) copy-start(bf16[64,512,128]{2,1,0:T(8,128)(2,1)S(1)} %shard_map.91.selector_ref) | copy-start | bytes 25165828

commit v6 on v5

--- a/solution.py
+++ b/solution.py
@@ -277,10 +277,10 @@
     two = one + one
 
     def expand(i, carry):
-        for pair in range(2):
+        for pair in range(4):
             tops = []
             for half in range(2):
-                block = 4 * i + 2 * pair + half
+                block = 8 * i + 2 * pair + half
                 sides = []
                 for side in range(2):
                     parts = []
@@ -291,7 +291,7 @@
                 top = jnp.concatenate([sides[0], empty], axis=1)
                 bottom = jnp.concatenate([empty, sides[1]], axis=1)
                 tops.append((block, jnp.concatenate([top, bottom], axis=0)))
-            at = pl.multiple_of((4 * i + 2 * pair) * BLOCK, 2 * BLOCK)
+            at = pl.multiple_of((8 * i + 2 * pair) * BLOCK, 2 * BLOCK)
             for c in range(sample_pairs // some):
                 even, odd = [], []
                 for block, rhs in tops:
@@ -315,9 +315,9 @@
             copies[part + AHEAD].start()
         if part == WEIGHTS_AT:
             weight_copy.start()
-        lax.fori_loop(part * share // 4, (part + 1) * share // 4, expand, 0)
-
-    per = 8
+        lax.fori_loop(part * share // 8, (part + 1) * share // 8, expand, 0)
+
+    per = 16
 
     def score(i, carry):
         mixing = compress_ref[...]
@@ -377,7 +377,7 @@
             pltpu.VMEM((groups * PACK_ROOM + most_rows, emb), jnp.float32),
             pltpu.VMEM((samples // 2, 2, features, emb), jnp.bfloat16),
             pltpu.VMEM((features // 128, mixes // BLOCK, samples * BLOCK, 128), jnp.float32),
-            pltpu.VMEM((4, 2 * emb, features), jnp.bfloat16),
+            pltpu.VMEM((8, 2 * emb, features), jnp.bfloat16),
             pltpu.VMEM(selectors.shape, jnp.bfloat16),
             pltpu.VMEM(weight.shape, jnp.bfloat16),
             pltpu.SemaphoreType.DMA((4,)),

time: 148 us -> 146 us (0.986)
  Pallas kernels: 73.2 us -> 71 us
    pallas_call x1, Pallas kernels: 20.2 us -> 18.1 us  [score_samples(): pl.pallas_call(functools.partial(tail_kernel, most_rows=most_rows), out_s...]
where the time goes in v6:
time: 146 us
  Pallas kernels  71 us (49%)
  blocking collectives  27.1 us (19%)
  waiting for transfers between devices  22.2 us (15%)
  local copies, waits for them, and re-layouts  15.6 us (11%)
  starting transfers between devices  7.61 us (5%)
  other arithmetic  1.91 us (1%)
    pallas_call x1, Pallas kernels, pool_rows(): pl.pallas_call(functools.partial(pool_kernel, first=first, rows=rows, poo...  27.9 us
    all_to_all x1, blocking collectives, shards(): lax.all_to_all(message, 'dev', split_axis=0, concat_axis=0, tiled=True)  27.1 us
    pallas_call x1, Pallas kernels, build_selectors(): pl.pallas_call(selector_kernel, grid=(blocks // some,), out_shape=jax.Sha...  23 us
    all_to_all x1, waiting for transfers between devices, shards(): lax.all_to_all(pooled, 'dev', split_axis=0, concat_axis=0, tiled=True)  22.2 us
    pallas_call x1, Pallas kernels, score_samples(): pl.pallas_call(functools.partial(tail_kernel, most_rows=most_rows), out_s...  18.1 us
    reshape x1, local copies, waits for them, and re-layouts, shards(): weight = jnp.transpose(top_weight.reshape(slots, mixes, -1), (1, 0, 2))  11.3 us
    all_to_all x1, starting transfers between devices, shards(): lax.all_to_all(pooled, 'dev', split_axis=0, concat_axis=0, tiled=True)  7.61 us
    unnamed x10, local copies, waits for them, and re-layouts  3.86 us
  transfers between devices with their start and end apart: 1, of which 1 were waited for; matrix products, arithmetic and copies ran while one was open for 10% of the time, Pallas kernels for 16%

profile of v6, /device:TPU:32, one launch (start us, length us, event | category | flops | bytes accessed | tf_op | source)
XLA Modules:
  0.0 145.8 jit_solution(200949899540835004)
XLA Ops:
  0.0 2.0 %shard_map.92 = s32[256,128]{1,0:T(8,128)} custom-call(s32[32,4,512]{2,1,0:T(4,128)} %bitcast.20, s32[32,512]{1,0:T(8,128)} %bitcast.22, s32[1,512]{1,0:T(1,128)} %counts_ref.1), custom_call_target="tpu_custom_call" | custom-call | tf_op jit(solution)/shard_map/pallas_call | solution.py:61
  2.0 27.1 %all_to_all.10 = s32[128,2,128]{2,1,0:T(2,128)} all-to-all(s32[128,2,128]{2,1,0:T(2,128)} %bitcast.19), channel_id=1, replica_groups=mesh['dev'=128,'rep'=2] {'dev'}, dimensions={0} | all-to-all | bytes 262144 | tf_op jit(solution)/shard_map/all_to_all | solution.py:401
  29.1 0.0 copy-start.2
  29.1 0.0 copy-start.1
  29.1 27.9 %shard_map.93 = bf16[128,80,128]{2,1,0:T(8,128)(2,1)} custom-call(s32[256,128]{1,0:T(8,128)} %bitcast.21, bf16[8192,128]{1,0:T(8,128)(2,1)} %bitcast.25), custom_call_target="tpu_custom_call" | custom-call | flops 20000000000 | bytes 5242880 | tf_op jit(solution)/shard_map/pallas_call | solution.py:158
  57.1 7.6 %all-to-all-start.1 = ((bf16[128,80,128]{2,1,0:T(8,128)(2,1)}), bf16[128,80,128]{2,1,0:T(8,128)(2,1)}, u32[]{:S(2)}, u32[]{:S(2)}) async-start(bf16[128,80,128]{2,1,0:T(8,128)(2,1)} %shard_map.93), calls=%async_computation.1 | async-start | bytes 5242880 | tf_op jit(solution)/shard_map/all_to_all | solution.py:404
  64.7 0.5 broadcast.37
  65.2 0.0 copy-done.2
  65.2 0.7 reduce.3
  65.9 0.1 reshape_squeeze.5
  66.0 0.2 reduce_window_sum.13
  66.2 0.1 reduce_window_sum.14
  66.3 0.1 add.32
  66.4 0.1 add.33
  66.5 0.0 copy-done.1
  66.5 0.1 copy.15
  66.6 0.0 copy-start.3
  66.6 11.3 %copy.19 = bf16[512,16,512]{2,0,1:T(8,128)(2,1)} copy(bf16[512,16,512]{2,1,0:T(8,128)(2,1)} %bitcast.17) | data formatting | bytes 16777216 | tf_op jit(solution)/shard_map/reshape | solution.py:417
  78.0 0.0 copy-done.3
  78.0 0.9 select_reduce_fusion
  78.9 0.2 convert_bitcast_fusion.pos_ref
  79.1 23.0 %shard_map.91.selector_ref = bf16[64,512,128]{2,1,0:T(8,128)(2,1)S(1)} custom-call(f32[512,128]{1,0:T(8,128)S(1)} %convert_bitcast_fusion.pos_ref), custom_call_target="tpu_custom_call" | custom-call | flops 10000000000 | bytes 8388608 | tf_op jit(solution)/shard_map/pallas_call | solution.py:215
  102.1 0.0 copy-start
  102.1 3.2 %copy-done = bf16[64,512,128]{2,1,0:T(8,128)(2,1)} copy-done((bf16[64,512,128]{2,1,0:T(8,128)(2,1)}, bf16[64,512,128]{2,1,0:T(8,128)(2,1)S(1)}, u32[]{:S(2)}) %copy-start) | copy-done | bytes 8388632
  105.3 22.2 %all-to-all-done.1.arrived_ref = bf16[128,80,128]{2,1,0:T(8,128)(2,1)} async-done(((bf16[128,80,128]{2,1,0:T(8,128)(2,1)}), bf16[128,80,128]{2,1,0:T(8,128)(2,1)}, u32[]{:S(2)}, u32[]{:S(2)}) %all-to-all-start.1) | async-done | bytes 2621472 | tf_op jit(solution)/shard_map/all_to_all | solution.py:404
  127.5 18.1 %shard_map.94 = bf16[128,512]{1,0:T(8,128)(2,1)} custom-call(s32[512]{0:T(512)} %get-tuple-element.6.base_ref, bf16[64,512,128]{2,1,0:T(8,128)(2,1)} %copy-done, bf16[16,512]{1,0:T(8,128)(2,1)} %compress_ref.1, bf16[16,512,512]{2,1,0:T(8,128)(2,1)} %bitcast.18, f32[1,512]{1,0:T(1,128)} %bitcast.26, bf16[128,80,128]{2,1,0:T(8,128)(2,1)} %all-to-all-done.1.arrived_ref), custom_call_target="tpu_custom_call" | custom-call | flops 20000000000 | bytes 16777216 | tf_op jit(solution)/shard_map/pallas_call | solution.py:370
  (3 shorter events, 0.0 us)
Async XLA Ops:
  29.1 36.1 %copy-start.2 = (s32[1,512]{1,0:T(1,128)S(1)}, s32[1,512]{1,0:T(1,128)}, u32[]{:S(2)}) copy-start(s32[1,512]{1,0:T(1,128)} %counts_ref.1) | copy-start | bytes 6148
  29.1 37.4 %copy-start.1 = (s32[128,512]{1,0:T(8,128)S(1)}, s32[128,512]{1,0:T(8,128)}, u32[]{:S(2)}) copy-start(s32[128,512]{1,0:T(8,128)} %param.13) | copy-start | bytes 786436
  57.1 70.4 %all-to-all-start.1 = ((bf16[128,80,128]{2,1,0:T(8,128)(2,1)}), bf16[128,80,128]{2,1,0:T(8,128)(2,1)}, u32[]{:S(2)}, u32[]{:S(2)}) async-start(bf16[128,80,128]{2,1,0:T(8,128)(2,1)} %shard_map.93), calls=%async_computation.1 | async-start | bytes 5242880 | tf_op jit(solution)/shard_map/all_to_all | solution.py:404
  66.6 11.4 %copy-start.3 = (s32[512]{0:T(512)S(1)}, s32[512]{0:T(512)}, u32[]{:S(2)}) copy-start(s32[512]{0:T(512)} %param.14) | copy-start | bytes 6148
  102.1 3.2 %copy-start = (bf16[64,512,128]{2,1,0:T(8,128)(2,1)}, bf16[64,512,128]{2,1,0:T(8,128)(2,1)S(1)}, u32[]{:S(2)}) copy-start(bf16[64,512,128]{2,1,0:T(8,128)(2,1)S(1)} %shard_map.91.selector_ref) | copy-start | bytes 25165828

commit v7 on v6

--- a/solution.py
+++ b/solution.py
@@ -13,7 +13,7 @@
 AHEAD = 3
 WEIGHTS_AT = 5
 SENDERS = 2
-SHARES = 8
+SHARES = 4
 GROUP = 4
 
 
@@ -317,7 +317,7 @@
             weight_copy.start()
         lax.fori_loop(part * share // 8, (part + 1) * share // 8, expand, 0)
 
-    per = 16
+    per = 32
 
     def score(i, carry):
         mixing = compress_ref[...]
@@ -377,7 +377,7 @@
             pltpu.VMEM((groups * PACK_ROOM + most_rows, emb), jnp.float32),
             pltpu.VMEM((samples // 2, 2, features, emb), jnp.bfloat16),
             pltpu.VMEM((features // 128, mixes // BLOCK, samples * BLOCK, 128), jnp.float32),
-            pltpu.VMEM((8, 2 * emb, features), jnp.bfloat16),
+            pltpu.VMEM((16, 2 * emb, features), jnp.bfloat16),
             pltpu.VMEM(selectors.shape, jnp.bfloat16),
             pltpu.VMEM(weight.shape, jnp.bfloat16),
             pltpu.SemaphoreType.DMA((4,)),

time: 146 us -> 146 us (level)
  no operation moved by 1% of the time
where the time goes in v7:
time: 146 us; the launch traced here: 145 us
  Pallas kernels  70.4 us (48%)
  blocking collectives  27.1 us (19%)
  waiting for transfers between devices  22.2 us (15%)
  local copies, waits for them, and re-layouts  15.6 us (11%)
  starting transfers between devices  7.61 us (5%)
  other arithmetic  1.91 us (1%)
    pallas_call x1, Pallas kernels, pool_rows(): pl.pallas_call(functools.partial(pool_kernel, first=first, rows=rows, poo...  27.9 us
    all_to_all x1, blocking collectives, shards(): lax.all_to_all(message, 'dev', split_axis=0, concat_axis=0, tiled=True)  27.1 us
    pallas_call x1, Pallas kernels, build_selectors(): pl.pallas_call(selector_kernel, grid=(blocks // some,), out_shape=jax.Sha...  23 us
    all_to_all x1, waiting for transfers between devices, shards(): lax.all_to_all(pooled, 'dev', split_axis=0, concat_axis=0, tiled=True)  22.2 us
    pallas_call x1, Pallas kernels, score_samples(): pl.pallas_call(functools.partial(tail_kernel, most_rows=most_rows), out_s...  17.5 us
    reshape x1, local copies, waits for them, and re-layouts, shards(): weight = jnp.transpose(top_weight.reshape(slots, mixes, -1), (1, 0, 2))  11.3 us
    all_to_all x1, starting transfers between devices, shards(): lax.all_to_all(pooled, 'dev', split_axis=0, concat_axis=0, tiled=True)  7.61 us
    unnamed x10, local copies, waits for them, and re-layouts  3.86 us
  transfers between devices with their start and end apart: 1, of which 1 were waited for; matrix products, arithmetic and copies ran while one was open for 10% of the time, Pallas kernels for 16%

profile of v7, /device:TPU:32, one launch (start us, length us, event | category | flops | bytes accessed | tf_op | source)
XLA Modules:
  0.0 145.2 jit_solution(8811466491570834642)
XLA Ops:
  0.0 2.0 %shard_map.92 = s32[256,128]{1,0:T(8,128)} custom-call(s32[32,4,512]{2,1,0:T(4,128)} %bitcast.20, s32[32,512]{1,0:T(8,128)} %bitcast.22, s32[1,512]{1,0:T(1,128)} %counts_ref.1), custom_call_target="tpu_custom_call" | custom-call | tf_op jit(solution)/shard_map/pallas_call | solution.py:61
  2.0 27.1 %all_to_all.10 = s32[128,2,128]{2,1,0:T(2,128)} all-to-all(s32[128,2,128]{2,1,0:T(2,128)} %bitcast.19), channel_id=1, replica_groups=mesh['dev'=128,'rep'=2] {'dev'}, dimensions={0} | all-to-all | bytes 262144 | tf_op jit(solution)/shard_map/all_to_all | solution.py:401
  29.1 0.0 copy-start.2
  29.1 0.0 copy-start.1
  29.1 27.9 %shard_map.93 = bf16[128,80,128]{2,1,0:T(8,128)(2,1)} custom-call(s32[256,128]{1,0:T(8,128)} %bitcast.21, bf16[8192,128]{1,0:T(8,128)(2,1)} %bitcast.25), custom_call_target="tpu_custom_call" | custom-call | flops 20000000000 | bytes 5242880 | tf_op jit(solution)/shard_map/pallas_call | solution.py:158
  57.1 7.6 %all-to-all-start.1 = ((bf16[128,80,128]{2,1,0:T(8,128)(2,1)}), bf16[128,80,128]{2,1,0:T(8,128)(2,1)}, u32[]{:S(2)}, u32[]{:S(2)}) async-start(bf16[128,80,128]{2,1,0:T(8,128)(2,1)} %shard_map.93), calls=%async_computation.1 | async-start | bytes 5242880 | tf_op jit(solution)/shard_map/all_to_all | solution.py:404
  64.7 0.5 broadcast.37
  65.2 0.0 copy-done.2
  65.2 0.7 reduce.3
  65.9 0.1 reshape_squeeze.5
  66.0 0.2 reduce_window_sum.13
  66.2 0.1 reduce_window_sum.14
  66.3 0.1 add.32
  66.4 0.1 add.33
  66.5 0.0 copy-done.1
  66.5 0.1 copy.15
  66.6 0.0 copy-start.3
  66.6 11.3 %copy.19 = bf16[512,16,512]{2,0,1:T(8,128)(2,1)} copy(bf16[512,16,512]{2,1,0:T(8,128)(2,1)} %bitcast.17) | data formatting | bytes 16777216 | tf_op jit(solution)/shard_map/reshape | solution.py:417
  78.0 0.0 copy-done.3
  78.0 0.9 select_reduce_fusion
  78.8 0.2 convert_bitcast_fusion.pos_ref
  79.0 23.0 %shard_map.91.selector_ref = bf16[64,512,128]{2,1,0:T(8,128)(2,1)S(1)} custom-call(f32[512,128]{1,0:T(8,128)S(1)} %convert_bitcast_fusion.pos_ref), custom_call_target="tpu_custom_call" | custom-call | flops 10000000000 | bytes 8388608 | tf_op jit(solution)/shard_map/pallas_call | solution.py:215
  102.0 0.0 copy-start
  102.1 3.2 %copy-done = bf16[64,512,128]{2,1,0:T(8,128)(2,1)} copy-done((bf16[64,512,128]{2,1,0:T(8,128)(2,1)}, bf16[64,512,128]{2,1,0:T(8,128)(2,1)S(1)}, u32[]{:S(2)}) %copy-start) | copy-done | bytes 8388632
  105.3 22.2 %all-to-all-done.1.arrived_ref = bf16[128,80,128]{2,1,0:T(8,128)(2,1)} async-done(((bf16[128,80,128]{2,1,0:T(8,128)(2,1)}), bf16[128,80,128]{2,1,0:T(8,128)(2,1)}, u32[]{:S(2)}, u32[]{:S(2)}) %all-to-all-start.1) | async-done | bytes 2621472 | tf_op jit(solution)/shard_map/all_to_all | solution.py:404
  127.5 17.5 %shard_map.94 = bf16[128,512]{1,0:T(8,128)(2,1)} custom-call(s32[512]{0:T(512)} %get-tuple-element.6.base_ref, bf16[64,512,128]{2,1,0:T(8,128)(2,1)} %copy-done, bf16[16,512]{1,0:T(8,128)(2,1)} %compress_ref.1, bf16[16,512,512]{2,1,0:T(8,128)(2,1)} %bitcast.18, f32[1,512]{1,0:T(1,128)} %bitcast.26, bf16[128,80,128]{2,1,0:T(8,128)(2,1)} %all-to-all-done.1.arrived_ref), custom_call_target="tpu_custom_call" | custom-call | flops 20000000000 | bytes 16777216 | tf_op jit(solution)/shard_map/pallas_call | solution.py:370
  (3 shorter events, 0.0 us)
Async XLA Ops:
  29.1 36.1 %copy-start.2 = (s32[1,512]{1,0:T(1,128)S(1)}, s32[1,512]{1,0:T(1,128)}, u32[]{:S(2)}) copy-start(s32[1,512]{1,0:T(1,128)} %counts_ref.1) | copy-start | bytes 6148
  29.1 37.3 %copy-start.1 = (s32[128,512]{1,0:T(8,128)S(1)}, s32[128,512]{1,0:T(8,128)}, u32[]{:S(2)}) copy-start(s32[128,512]{1,0:T(8,128)} %param.13) | copy-start | bytes 786436
  57.1 70.4 %all-to-all-start.1 = ((bf16[128,80,128]{2,1,0:T(8,128)(2,1)}), bf16[128,80,128]{2,1,0:T(8,128)(2,1)}, u32[]{:S(2)}, u32[]{:S(2)}) async-start(bf16[128,80,128]{2,1,0:T(8,128)(2,1)} %shard_map.93), calls=%async_computation.1 | async-start | bytes 5242880 | tf_op jit(solution)/shard_map/all_to_all | solution.py:404
  66.6 11.4 %copy-start.3 = (s32[512]{0:T(512)S(1)}, s32[512]{0:T(512)}, u32[]{:S(2)}) copy-start(s32[512]{0:T(512)} %param.14) | copy-start | bytes 6148
  102.0 3.2 %copy-start = (bf16[64,512,128]{2,1,0:T(8,128)(2,1)}, bf16[64,512,128]{2,1,0:T(8,128)(2,1)S(1)}, u32[]{:S(2)}) copy-start(bf16[64,512,128]{2,1,0:T(8,128)(2,1)S(1)} %shard_map.91.selector_ref) | copy-start | bytes 25165828
